TPU v7x, 32 devices: a whole 2x2x4 slice. The times are simulated.
32 devices in a mesh: band: 16 (over z, x, core), lev: 2 (over y).
Axes of the slice: x: 2, y: 2, z: 4, core: 2. Of those that a mesh axis runs over, the one named last changes fastest.
Arguments:
- field_grid: float32 [3, 8, 384, 2, 1536], P(None, 'lev', 'band'), may hold values from -6 to 6
- increment: float32 [3, 8, 384, 2, 1536], P(None, 'lev', 'band'), may hold values from -6 to 6
- points: int32 [384], P('band'), may hold values from 16 to 1536, as said below
- weights: float32 [384], replicated, may hold values from 0.0013020834 to 0.0052083335
- pair_slot: int32 [384], replicated, may hold values from 0 to 383, each once
- legendre: float32 [384, 384, 769], P(('band', 'lev')), may hold values from -6 to 6
- strength: float32 [3, 8], replicated, may hold values from 1 to 16
Outputs:
- stepped: float32 [3, 8, 384, 2, 1536], P(None, 'lev', 'band')
Inputs may be any that keep to these rules, and one draw needn't show every extreme that they name: points[j] lies within 32 of 16 + 1520 * j // 383, kept within 16 to 1536; the last latitude pair has 1536 cells. `pair_slot`: A permutation of 0 to 383; slot s is held by the device of joint band+lev index s // 12, at place s % 12, which holds legendre[s].
All inputs are finite; a program needn't handle non-finite values.
Results may differ from a plain program's by a relative error of at most 0.0003.
Values sent between devices are 32-bit elements; how exact they have to be, the bound alone decides.
A program may use at most 320 MiB of HBM per device.

v0:
```python
import functools
import math

import jax
import jax.numpy as jnp
from jax import lax
from jax.experimental import pallas as pl
from jax.experimental.pallas import tpu as pltpu
from jax.sharding import PartitionSpec as P

LANES = 128
SPAN = 256
FINE = 16
MIB = 1024 * 1024
SINE = [(-1) ** k * math.pi ** (2 * k + 1) / math.factorial(2 * k + 1) for k in range(6)]
COSINE = [(-1) ** k * math.pi ** (2 * k) / math.factorial(2 * k) for k in range(7)]


def halves(values):
    high = values.astype(jnp.bfloat16)
    return high, (values - high.astype(jnp.float32)).astype(jnp.bfloat16)


def iota(shape, dim):
    return lax.broadcasted_iota(jnp.int32, shape, dim)


def turn(product, count, inverse):
    whole = jnp.floor(product * inverse + 0.5)
    part = (product - whole * count) * inverse
    square = part * part
    sine, cosine = SINE[-1], COSINE[-1]
    for term in SINE[-2::-1]:
        sine = sine * square + term
    for term in COSINE[-2::-1]:
        cosine = cosine * square + term
    sine = sine * part
    return 1.0 - 2.0 * sine * sine, 2.0 * sine * cosine


def dot(left, right):
    return lax.dot_general(
        left, right, (((1,), (0,)), ((), ())), preferred_element_type=jnp.float32
    )


def mirror(values):
    lane = iota(values.shape, 1)
    width = values.shape[1]
    return jnp.where(
        lane % 2 == 0,
        values + pltpu.roll(values, width - 1, 1),
        pltpu.roll(values, 1, 1) - values,
    )


def wave_at(pairs, place, waves):
    lower = pairs[place // 2]
    return jnp.where(place % 2 == 0, lower, waves - 1 - lower)


def forward_kernel(
    counts, pairs, field_ref, more_ref, out_ref, row_ref, high_ref, low_ref, wave_ref, *, stride
):
    fields, local, _, _, length = field_ref.shape
    devices, _, groups, lats, _ = out_ref.shape
    waves = length // 2
    rows = fields * local * 2
    each = 2 * local
    wide = 2 * each
    group = 2 * (waves // 2 // devices) // groups
    blocks = length // SPAN
    lat = pl.program_id(0)
    count = counts[lat]
    real = count.astype(jnp.float32)
    inverse = 1.0 / jnp.full((1, 1), real, jnp.float32)
    for f in range(fields):
        for l in range(local):
            row_ref[pl.ds((f * local + l) * 2, 2), :] = field_ref[f, l, 0] + more_ref[f, l, 0]
    pieces = []
    for b in range(blocks):
        piece = row_ref[:, b * SPAN : (b + 1) * SPAN]
        place = b * SPAN + iota(piece.shape, 1)
        pieces.append(jnp.where(place < count, piece, 0.0))
    high, low = halves(jnp.concatenate(pieces, axis=0))
    both = jnp.concatenate([high, low], axis=0)
    total = blocks * rows
    for q in range(waves // SPAN):
        order = q * SPAN + iota((1, SPAN), 1)
        order = order.astype(jnp.float32)
        steps = iota((FINE, SPAN), 0).astype(jnp.float32)
        fine_cos, fine_sin = turn(steps * order, real, inverse)
        coarse_cos, coarse_sin = turn(FINE * steps * order, real, inverse)
        block_cos, block_sin = turn(SPAN * steps[:8] * order, real, inverse)
        for i in range(SPAN // FINE):
            cosine, sine = coarse_cos[i : i + 1], coarse_sin[i : i + 1]
            place = pl.ds(i * FINE, FINE)
            top, rest = halves(cosine * fine_cos - sine * fine_sin)
            high_ref[q, place, :SPAN] = top
            low_ref[q, place, :SPAN] = rest
            top, rest = halves(sine * fine_cos + cosine * fine_sin)
            high_ref[q, place, SPAN:] = top
            low_ref[q, place, SPAN:] = rest
        first = dot(both, high_ref[q])
        product = first[:total] + (first[total:] + dot(high, low_ref[q]))
        real_part = jnp.zeros((rows, SPAN), jnp.float32)
        imaginary = jnp.zeros((rows, SPAN), jnp.float32)
        for b in range(blocks):
            in_cos = product[b * rows : (b + 1) * rows, :SPAN]
            in_sin = product[b * rows : (b + 1) * rows, SPAN:]
            cosine, sine = block_cos[b : b + 1], block_sin[b : b + 1]
            real_part += cosine * in_cos - sine * in_sin
            imaginary -= sine * in_cos + cosine * in_sin
        live = order.astype(jnp.int32) <= (count - 1) // 2
        scale = jnp.where(live, inverse, 0.0)
        real_part, imaginary = real_part * scale, imaginary * scale
        parts = []
        for f in range(fields):
            parts += [real_part[f * each : (f + 1) * each], imaginary[f * each : (f + 1) * each]]
        parts.append(jnp.zeros((LANES - fields * wide, SPAN), jnp.float32))
        turned = jnp.concatenate(parts, axis=0).T
        wave_ref[pl.ds(q * SPAN * stride + lat, SPAN, stride=stride), :] = turned

    @pl.when(lat == pl.num_programs(0) - 1)
    def _():
        lane = iota((lats, LANES), 1) // wide

        def assemble(index, carry):
            device, part = index // groups, index % groups
            outs = [jnp.zeros((lats, LANES), jnp.float32)] * fields
            for i in range(group):
                wave = wave_at(pairs, index * group + i, waves)
                value = wave_ref[pl.ds(pl.multiple_of(wave * stride, 8), lats), :]
                for f in range(fields):
                    moved = pltpu.roll(value, (i - f) * wide % LANES, 1)
                    outs[f] = jnp.where(lane == i, moved, outs[f])
            for f in range(fields):
                out_ref[device, f, part] = outs[f]
            return carry

        lax.fori_loop(0, devices * groups, assemble, 0)


def inverse_kernel(
    counts, pairs, come_ref, out_ref, high_ref, low_ref, wave_ref, *, stride
):
    fields, local, _, _, length = out_ref.shape
    devices, _, groups, lats, _ = come_ref.shape
    waves = length // 2
    rows = fields * local * 2
    each = 2 * local
    wide = 2 * each
    group = 2 * (waves // 2 // devices) // groups
    blocks = length // SPAN
    lat = pl.program_id(0)
    count = counts[lat]
    real = count.astype(jnp.float32)
    inverse = 1.0 / jnp.full((1, 1), real, jnp.float32)

    @pl.when(lat == 0)
    def _():
        lane = iota((lats, LANES), 1) // wide

        def spread(index, carry):
            device, part = index // groups, index % groups
            values = [come_ref[device, f, part] for f in range(fields)]
            for i in range(group):
                wave = wave_at(pairs, index * group + i, waves)
                out = jnp.zeros((lats, LANES), jnp.float32)
                for f in range(fields):
                    moved = pltpu.roll(values[f], (f - i) * wide % LANES, 1)
                    out = jnp.where(lane == f, moved, out)
                wave_ref[pl.ds(pl.multiple_of(wave * stride, 8), lats), :] = out
            return carry

        lax.fori_loop(0, devices * groups, spread, 0)

    total = blocks * rows
    result = jnp.zeros((total, SPAN), jnp.float32)
    place = iota((1, SPAN), 1).astype(jnp.float32)
    steps = iota((FINE, SPAN), 0).astype(jnp.float32)
    fine_cos, fine_sin = turn(steps * place, real, inverse)
    for q in range(waves // SPAN):
        start = float(q * SPAN)
        coarse_cos, coarse_sin = turn((start + FINE * steps) * place, real, inverse)
        order = start + place
        block_cos, block_sin = turn(SPAN * steps[:8] * order, real, inverse)
        for i in range(SPAN // FINE):
            cosine, sine = coarse_cos[i : i + 1], coarse_sin[i : i + 1]
            top, rest = halves(cosine * fine_cos - sine * fine_sin)
            high_ref[q, i * FINE : (i + 1) * FINE] = top
            low_ref[q, i * FINE : (i + 1) * FINE] = rest
            top, rest = halves(-(sine * fine_cos + cosine * fine_sin))
            high_ref[q, SPAN + i * FINE : SPAN + (i + 1) * FINE] = top
            low_ref[q, SPAN + i * FINE : SPAN + (i + 1) * FINE] = rest
        turned = wave_ref[pl.ds(q * SPAN * stride + lat, SPAN, stride=stride), :].T
        real_part = jnp.concatenate(
            [turned[f * wide : f * wide + each] for f in range(fields)], axis=0
        )
        imaginary = jnp.concatenate(
            [turned[f * wide + each : (f + 1) * wide] for f in range(fields)], axis=0
        )
        wave = order.astype(jnp.int32)
        double = jnp.where(wave == 0, 1.0, 2.0)
        double = jnp.where(wave <= (count - 1) // 2, double, 0.0)
        block_cos, block_sin = block_cos * double, block_sin * double
        shifted = []
        for b in range(blocks):
            cosine, sine = block_cos[b : b + 1], block_sin[b : b + 1]
            shifted.append(
                jnp.concatenate(
                    [real_part * cosine - imaginary * sine, real_part * sine + imaginary * cosine],
                    axis=1,
                )
            )
        high, low = halves(jnp.concatenate(shifted, axis=0))
        first = dot(jnp.concatenate([high, low], axis=0), high_ref[q])
        result += first[:total] + (first[total:] + dot(high, low_ref[q]))
    for b in range(blocks):
        live = b * SPAN + iota((rows, SPAN), 1) < count
        piece = jnp.where(live, result[b * rows : (b + 1) * rows], 0.0)
        for f in range(fields):
            for l in range(local):
                start = (f * local + l) * 2
                out_ref[f, l, 0, :, b * SPAN : (b + 1) * SPAN] = piece[start : start + 2]


def table_kernel(table_ref, weight_ref, high_ref, low_ref, high_t_ref, low_t_ref, pad_ref):
    columns = table_ref.shape[2]
    padded = pad_ref.shape[1]
    kept = high_t_ref.shape[1]
    pad_ref[:, padded - LANES :] = jnp.zeros((pad_ref.shape[0], LANES), jnp.float32)
    pad_ref[:, :columns] = table_ref[0]
    values = pad_ref[...]
    high_ref[0], low_ref[0] = halves(values)
    turned = values.T[:kept] * weight_ref[...]
    high_t_ref[0], low_t_ref[0] = halves(turned)


def legendre_kernel(
    lowers, come_ref, high_ref, low_ref, high_t_ref, low_t_ref, rate_ref, out_ref, data_ref, damp_ref,
    *, lev, waves, member
):
    slot = pl.program_id(0)
    devices, fields, _, lats, _ = come_ref.shape
    bands = devices // lev
    size = 2 * member
    per_tile = LANES // size
    pieces = lev * fields
    tiles = -(-pieces // per_tile)
    width = tiles * LANES
    lower = lowers[slot]
    spot = lowers[pl.num_programs(0) + slot]
    lane_piece = iota((lats, LANES), 1) // size
    for band in range(bands):
        for t in range(tiles):
            value = jnp.zeros((lats, LANES), jnp.float32)
            for k in range(t * per_tile, min((t + 1) * per_tile, pieces)):
                piece = come_ref[band * lev + k // fields, k % fields, 0]
                shift = lax.rem((k % per_tile) * size - spot * size + LANES, LANES)
                value = jnp.where(lane_piece == k % per_tile, pltpu.roll(piece, shift, 1), value)
            data_ref[pl.ds(band * lats, lats), t * LANES : (t + 1) * LANES] = value
    high, low = halves(mirror(data_ref[...]))
    kept = high_t_ref.shape[1]
    first = dot(high_t_ref[0], jnp.concatenate([high, low], axis=1))
    analysed = first[:, :width] + (first[:, width:] + dot(low_t_ref[0], high))
    column = iota((kept, 1), 0)
    second = column >= waves - lower
    degree = jnp.where(second, column - 1, lower + column)
    order = jnp.where(second, waves - 1 - lower, lower)
    odd = (degree - order) & 1
    code = jnp.where(column <= waves, 2 * second.astype(jnp.int32) + odd, -1)
    degree = degree.astype(jnp.float32)
    ratio = degree * (degree + 1.0) * (1.0 / float((waves - 1) * waves))
    square = ratio * ratio
    lane = iota((1, width), 1)
    mine = (lane // member % 2) * 2 + lane % 2
    damped = jnp.where(code == mine, analysed / (1.0 + rate_ref[...] * square), 0.0)
    damp_ref[:kept] = damped
    damp_ref[kept:] = jnp.zeros((damp_ref.shape[0] - kept, width), jnp.float32)
    high, low = halves(damp_ref[...])
    first = dot(high_ref[0], jnp.concatenate([high, low], axis=1))
    back = first[:, :width] + (first[:, width:] + dot(low_ref[0], high))
    data_ref[...] = mirror(back)

    @pl.when(spot == 0)
    def _():
        out_ref[...] = jnp.zeros_like(out_ref)

    for band in range(bands):
        for k in range(pieces):
            t = k // per_tile
            piece = data_ref[pl.ds(band * lats, lats), t * LANES : (t + 1) * LANES]
            shift = lax.rem(spot * size - (k % per_tile) * size + LANES, LANES)
            target = (band * lev + k // fields, k % fields, 0)
            out_ref[target] = jnp.where(lane_piece == spot, pltpu.roll(piece, shift, 1), out_ref[target])


def body(field_grid, increment, points, weights, pair_slot, legendre, strength):
    bands = lax.axis_size("band")
    lev = lax.axis_size("lev")
    devices = bands * lev
    fields, local, lats, _, length = field_grid.shape
    waves = length // 2
    slots, half, columns = legendre.shape
    member = 4 * local
    pair_count = waves // 2
    ranks = lax.iota(jnp.int32, pair_count)
    pairs = jnp.sum(jnp.where(pair_slot[None, :] == ranks[:, None], ranks[None, :], 0), axis=1)
    group = max(
        g for g in range(2, 2 * slots + 1, 2) if 2 * slots % g == 0 and g * member <= LANES
    )
    groups = 2 * slots // group
    stride = -(-lats // 8) * 8
    blocks = length // SPAN
    rows = fields * local * 2
    grid_block = pl.BlockSpec((fields, local, 1, 2, length), lambda j, *_: (0, 0, j, 0, 0))
    buffer = (devices, fields, groups, lats, LANES)
    whole_block = pl.BlockSpec(buffer, lambda j, *_: (0, 0, 0, 0, 0))
    waved = pltpu.VMEM((waves * stride, LANES), jnp.float32)
    flops = lats * 6 * blocks * rows * SPAN * length
    sent = pl.pallas_call(
        functools.partial(forward_kernel, stride=stride),
        out_shape=jax.ShapeDtypeStruct(buffer, jnp.float32),
        grid_spec=pltpu.PrefetchScalarGridSpec(
            num_scalar_prefetch=2,
            grid=(lats,),
            in_specs=[grid_block, grid_block],
            out_specs=whole_block,
            scratch_shapes=[
                pltpu.VMEM((rows, length), jnp.float32),
                pltpu.VMEM((waves // SPAN, SPAN, 2 * SPAN), jnp.bfloat16),
                pltpu.VMEM((waves // SPAN, SPAN, 2 * SPAN), jnp.bfloat16),
                waved,
            ],
        ),
        cost_estimate=pl.CostEstimate(flops=flops, bytes_accessed=0, transcendentals=0),
    )(points, pairs, field_grid, increment)
    arrived = lax.all_to_all(sent, ("band", "lev"), split_axis=0, concat_axis=0, tiled=True)

    padded = -(-columns // LANES) * LANES
    kept = -(-columns // 16) * 16
    plain = pl.BlockSpec((1, half, padded), lambda s, *_: (s, 0, 0))
    turned = pl.BlockSpec((1, kept, half), lambda s, *_: (s, 0, 0))
    tables = pl.pallas_call(
        table_kernel,
        out_shape=[jax.ShapeDtypeStruct((slots, half, padded), jnp.bfloat16)] * 2
        + [jax.ShapeDtypeStruct((slots, kept, half), jnp.bfloat16)] * 2,
        grid=(slots,),
        in_specs=[
            pl.BlockSpec((1, half, columns), lambda s: (s, 0, 0)),
            pl.BlockSpec((1, half), lambda s: (0, 0)),
        ],
        out_specs=[plain, plain, turned, turned],
        scratch_shapes=[pltpu.VMEM((half, padded), jnp.float32)],
        cost_estimate=pl.CostEstimate(
            flops=slots * 4 * half * padded * 256, bytes_accessed=0, transcendentals=0
        ),
    )(legendre, weights[None, :])

    size = 2 * member
    per_tile = LANES // size
    tiles = -(-lev * fields // per_tile)
    width = tiles * LANES
    rate = jnp.moveaxis(strength.reshape(fields, lev, local), 1, 0)
    rate = jnp.broadcast_to(rate[:, :, None, :, None], (lev, fields, 4, local, 2)).reshape(1, -1)
    rate = jnp.pad(rate, ((0, 0), (0, width - rate.shape[1])))
    own = lax.dynamic_slice_in_dim(pairs, lax.axis_index(("band", "lev")) * slots, slots)
    per_group = group // 2
    lowers = jnp.concatenate([own, lax.iota(jnp.int32, slots) % per_group])
    mail = pl.BlockSpec((devices, fields, 1, lats, LANES), lambda s, *_: (0, 0, s // per_group, 0, 0))
    returned = pl.pallas_call(
        functools.partial(legendre_kernel, lev=lev, waves=waves, member=member),
        out_shape=jax.ShapeDtypeStruct(buffer, jnp.float32),
        grid_spec=pltpu.PrefetchScalarGridSpec(
            num_scalar_prefetch=1,
            grid=(slots,),
            in_specs=[
                mail, plain, plain, turned, turned,
                pl.BlockSpec((1, width), lambda s, *_: (0, 0)),
            ],
            out_specs=mail,
            scratch_shapes=[
                pltpu.VMEM((half, width), jnp.float32),
                pltpu.VMEM((padded, width), jnp.float32),
            ],
        ),
        cost_estimate=pl.CostEstimate(
            flops=slots * 12 * half * padded * width, bytes_accessed=0, transcendentals=0
        ),
    )(lowers, arrived, *tables, rate)
    home = lax.all_to_all(returned, ("band", "lev"), split_axis=0, concat_axis=0, tiled=True)

    return pl.pallas_call(
        functools.partial(inverse_kernel, stride=stride),
        out_shape=jax.ShapeDtypeStruct(field_grid.shape, jnp.float32),
        grid_spec=pltpu.PrefetchScalarGridSpec(
            num_scalar_prefetch=2,
            grid=(lats,),
            in_specs=[whole_block],
            out_specs=grid_block,
            scratch_shapes=[
                pltpu.VMEM((waves // SPAN, 2 * SPAN, SPAN), jnp.bfloat16),
                pltpu.VMEM((waves // SPAN, 2 * SPAN, SPAN), jnp.bfloat16),
                waved,
            ],
        ),
        cost_estimate=pl.CostEstimate(flops=flops, bytes_accessed=0, transcendentals=0),
    )(points, pairs, home)


def solution(mesh):
    return jax.shard_map(
        body,
        mesh=mesh,
        in_specs=(
            P(None, "lev", "band", None, None),
            P(None, "lev", "band", None, None),
            P("band"),
            P(),
            P(),
            P(("band", "lev"), None, None),
            P(),
        ),
        out_specs=P(None, "lev", "band", None, None),
        check_vma=False,
    )
```

profile of v0, /device:TPU:27, one launch (start us, length us, event | category | flops | bytes accessed | tf_op | source)
XLA Modules:
  0.0 298.7 jit_solution(3142200305419855792)
XLA Ops:
  0.0 1.4 select_reduce_fusion.pairs
  1.4 40.7 %shard_map.73 = f32[32,3,3,24,128]{4,3,2,1,0:T(8,128)} custom-call(s32[24]{0:T(128)} %counts.3, s32[384]{0:T(512)} %select_reduce_fusion.pairs, f32[3,4,24,2,1536]{4,3,2,1,0:T(2,128)} %field_ref.1, f32[3,4,24,2,1536]{4,3,2,1,0:T(2,128)} %more_ref.1), custom_call_target="tpu_custom_call" | custom-call | flops 8153726976 | tf_op jit(solution)/shard_map/pallas_call | solution.py:322
  42.1 6.1 %all-to-all-start = ((f32[32,3,3,24,128]{4,3,2,1,0:T(8,128)}), f32[32,3,3,24,128]{4,3,2,1,0:T(8,128)S(1)}, u32[]{:S(2)}, u32[]{:S(2)}) async-start(f32[32,3,3,24,128]{4,3,2,1,0:T(8,128)} %shard_map.73), calls=%async_computation | async-start | bytes 7077888 | tf_op jit(solution)/shard_map/all_to_all | solution.py:339
  48.3 0.7 dynamic_slice.3
  49.0 0.0 copy-start.1
  49.0 0.0 copy-start.2
  49.0 16.3 %copy.12.table_ref = f32[12,384,769]{2,1,0:T(8,128)} copy(f32[12,384,769]{1,2,0:T(8,128)} %param.12) | data formatting | bytes 28348416 | tf_op args[5]
  65.3 0.0 copy-done.1
  65.3 0.6 broadcast_in_dim.26.weight_ref
  65.9 0.0 copy-done.2
  65.9 0.1 reshape.8
  66.0 0.7 broadcast_in_dim.27
  66.7 0.9 reshape.9
  67.6 0.6 pad.4.rate_ref
  68.2 0.7 pad_add_fusion.lowers
  68.9 18.9 %shard_map.74 = (bf16[12,384,896]{2,1,0:T(8,128)(2,1)}, bf16[12,384,896]{2,1,0:T(8,128)(2,1)}, bf16[12,784,384]{2,1,0:T(8,128)(2,1)}, bf16[12,784,384]{2,1,0:T(8,128)(2,1)}) custom-call(f32[12,384,769]{2,1,0:T(8,128)} %copy.12.table_ref, f32[1,384]{1,0:T(1,128)} %broadcast_in_dim.26.weight_ref), custom_call_target="tpu_custom_call" | custom-call | flops 4227858432 | tf_op jit(solution)/shard_map/pallas_call | solution.py:345
  87.8 38.0 %all-to-all-done.come_ref = f32[32,3,3,24,128]{4,3,2,1,0:T(8,128)S(1)} async-done(((f32[32,3,3,24,128]{4,3,2,1,0:T(8,128)}), f32[32,3,3,24,128]{4,3,2,1,0:T(8,128)S(1)}, u32[]{:S(2)}, u32[]{:S(2)}) %all-to-all-start) | async-done | bytes 3538976 | tf_op jit(solution)/shard_map/all_to_all | solution.py:339
  125.8 0.0 copy-start
  125.8 1.8 copy-done
  127.6 48.4 %shard_map.75 = f32[32,3,3,24,128]{4,3,2,1,0:T(8,128)} custom-call(s32[24]{0:T(128)} %pad_add_fusion.lowers, f32[32,3,3,24,128]{4,3,2,1,0:T(8,128)} %copy-done, bf16[12,384,896]{2,1,0:T(8,128)(2,1)} %get-tuple-element.9.high_ref, bf16[12,384,896]{2,1,0:T(8,128)(2,1)} %get-tuple-element.10.low_ref, bf16[12,784,384]{2,1,0:T(8,128)(2,1)} %get-tuple-element.11.high_t_ref, ...), custom_call_target="tpu_custom_call" | custom-call | flops 12683575296 | tf_op jit(solution)/shard_map/pallas_call | solution.py:372
  176.0 83.7 %all_to_all.10.come_ref = f32[32,3,3,24,128]{4,3,2,1,0:T(8,128)} all-to-all(f32[32,3,3,24,128]{4,3,2,1,0:T(8,128)} %shard_map.75), channel_id=1, replica_groups=mesh['band'=16,'lev'=2] {'band','lev'}, dimensions={0} | all-to-all | bytes 7077888 | tf_op jit(solution)/shard_map/all_to_all | solution.py:392
  259.7 39.0 %shard_map.76 = f32[3,4,24,2,1536]{4,3,2,1,0:T(2,128)} custom-call(s32[24]{0:T(128)} %counts.3, s32[384]{0:T(512)} %select_reduce_fusion.pairs, f32[32,3,3,24,128]{4,3,2,1,0:T(8,128)} %all_to_all.10.come_ref), custom_call_target="tpu_custom_call" | custom-call | flops 8153726976 | tf_op jit(solution)/shard_map/pallas_call | solution.py:394
  (2 shorter events, 0.0 us)
Async XLA Ops:
  42.1 83.7 %all-to-all-start = ((f32[32,3,3,24,128]{4,3,2,1,0:T(8,128)}), f32[32,3,3,24,128]{4,3,2,1,0:T(8,128)S(1)}, u32[]{:S(2)}, u32[]{:S(2)}) async-start(f32[32,3,3,24,128]{4,3,2,1,0:T(8,128)} %shard_map.73), calls=%async_computation | async-start | bytes 7077888 | tf_op jit(solution)/shard_map/all_to_all | solution.py:339
  49.0 16.3 %copy-start.1 = (f32[384]{0:T(512)S(1)}, f32[384]{0:T(512)}, u32[]{:S(2)}) copy-start(f32[384]{0:T(512)} %param.10) | copy-start | bytes 4612
  49.0 16.9 %copy-start.2 = (f32[3,8]{1,0:T(4,128)S(1)}, f32[3,8]{1,0:T(4,128)}, u32[]{:S(2)}) copy-start(f32[3,8]{1,0:T(4,128)} %param.13) | copy-start | bytes 292
  125.8 1.8 copy-start
where the time goes:
time: 304 us; the launch traced here: 299 us
  Pallas kernels  147 us (48%)
  blocking collectives  83.7 us (28%)
  waiting for transfers between devices  38 us (12%)
  local copies, waits for them, and re-layouts  21.7 us (7%)
  starting transfers between devices  6.14 us (2%)
    all_to_all x1, blocking collectives, body(): lax.all_to_all(returned, ('band', 'lev'), split_axis=0, concat_axis=0, ti...  83.7 us
    pallas_call x1, Pallas kernels, body(): pl.pallas_call(functools.partial(legendre_kernel, lev=lev, waves=waves, m...  48.4 us
    pallas_call x1, Pallas kernels, body(): pl.pallas_call(functools.partial(forward_kernel, stride=stride), out_shap...  40.7 us
    pallas_call x1, Pallas kernels, body(): pl.pallas_call(functools.partial(inverse_kernel, stride=stride), out_shap...  39 us
    all_to_all x1, waiting for transfers between devices, body(): lax.all_to_all(sent, ('band', 'lev'), split_axis=0, concat_axis=0, tiled=...  38 us
    pallas_call x1, Pallas kernels, body(): pl.pallas_call(table_kernel, out_shape=[jax.ShapeDtypeStruct((slots, half...  18.9 us
    unnamed x7, local copies, waits for them, and re-layouts  18.1 us
    all_to_all x1, starting transfers between devices, body(): lax.all_to_all(sent, ('band', 'lev'), split_axis=0, concat_axis=0, tiled=...  6.14 us
  transfers between devices with their start and end apart: 1, of which 1 were waited for; matrix products, arithmetic and copies ran while one was open for 7% of the time, Pallas kernels for 6%

commit v1 on v0

--- a/solution.py
+++ b/solution.py
@@ -3,6 +3,7 @@
 
 import jax
 import jax.numpy as jnp
+import numpy as np
 from jax import lax
 from jax.experimental import pallas as pl
 from jax.experimental.pallas import tpu as pltpu
@@ -11,7 +12,7 @@
 LANES = 128
 SPAN = 256
 FINE = 16
-MIB = 1024 * 1024
+SEATS = 4
 SINE = [(-1) ** k * math.pi ** (2 * k + 1) / math.factorial(2 * k + 1) for k in range(6)]
 COSINE = [(-1) ** k * math.pi ** (2 * k) / math.factorial(2 * k) for k in range(7)]
 
@@ -54,21 +55,16 @@
     )
 
 
-def wave_at(pairs, place, waves):
-    lower = pairs[place // 2]
-    return jnp.where(place % 2 == 0, lower, waves - 1 - lower)
-
-
 def forward_kernel(
     counts, pairs, field_ref, more_ref, out_ref, row_ref, high_ref, low_ref, wave_ref, *, stride
 ):
     fields, local, _, _, length = field_ref.shape
-    devices, _, groups, lats, _ = out_ref.shape
+    chunks, devices, tiles, lats, _ = out_ref.shape
     waves = length // 2
     rows = fields * local * 2
     each = 2 * local
     wide = 2 * each
-    group = 2 * (waves // 2 // devices) // groups
+    group = waves // 2 // devices // chunks
     blocks = length // SPAN
     lat = pl.program_id(0)
     count = counts[lat]
@@ -126,31 +122,35 @@
         lane = iota((lats, LANES), 1) // wide
 
         def assemble(index, carry):
-            device, part = index // groups, index % groups
-            outs = [jnp.zeros((lats, LANES), jnp.float32)] * fields
-            for i in range(group):
-                wave = wave_at(pairs, index * group + i, waves)
-                value = wave_ref[pl.ds(pl.multiple_of(wave * stride, 8), lats), :]
-                for f in range(fields):
-                    moved = pltpu.roll(value, (i - f) * wide % LANES, 1)
-                    outs[f] = jnp.where(lane == i, moved, outs[f])
-            for f in range(fields):
-                out_ref[device, f, part] = outs[f]
+            chunk, device = index // devices, index % devices
+            outs = [jnp.zeros((lats, LANES), jnp.float32)] * tiles
+            for s in range(group):
+                lower = pairs[device * chunks * group + chunk * group + s]
+                for member in range(2):
+                    wave = lower if member == 0 else waves - 1 - lower
+                    value = wave_ref[pl.ds(pl.multiple_of(wave * stride, 8), lats), :]
+                    for f in range(fields):
+                        unit = member * fields + f
+                        spot = unit % 2 * SEATS + s
+                        moved = pltpu.roll(value, (spot - f) * wide % LANES, 1)
+                        outs[unit // 2] = jnp.where(lane == spot, moved, outs[unit // 2])
+            for t in range(tiles):
+                out_ref[chunk, device, t] = outs[t]
             return carry
 
-        lax.fori_loop(0, devices * groups, assemble, 0)
+        lax.fori_loop(0, devices * chunks, assemble, 0)
 
 
 def inverse_kernel(
-    counts, pairs, come_ref, out_ref, high_ref, low_ref, wave_ref, *, stride
+    counts, pairs, come_ref, out_ref, high_ref, low_ref, wave_ref, *, stride, light, short
 ):
     fields, local, _, _, length = out_ref.shape
-    devices, _, groups, lats, _ = come_ref.shape
+    chunks, devices, tiles, lats, _ = come_ref.shape
     waves = length // 2
     rows = fields * local * 2
     each = 2 * local
     wide = 2 * each
-    group = 2 * (waves // 2 // devices) // groups
+    group = waves // 2 // devices // chunks
     blocks = length // SPAN
     lat = pl.program_id(0)
     count = counts[lat]
@@ -160,20 +160,27 @@
     @pl.when(lat == 0)
     def _():
         lane = iota((lats, LANES), 1) // wide
+        small = lax.axis_index("band") < light
 
         def spread(index, carry):
-            device, part = index // groups, index % groups
-            values = [come_ref[device, f, part] for f in range(fields)]
-            for i in range(group):
-                wave = wave_at(pairs, index * group + i, waves)
-                out = jnp.zeros((lats, LANES), jnp.float32)
-                for f in range(fields):
-                    moved = pltpu.roll(values[f], (f - i) * wide % LANES, 1)
-                    out = jnp.where(lane == f, moved, out)
-                wave_ref[pl.ds(pl.multiple_of(wave * stride, 8), lats), :] = out
+            chunk, device = index // devices, index % devices
+            values = [come_ref[chunk, device, t] for t in range(tiles)]
+            for t in range(short, tiles):
+                values[t] = jnp.where(small, 0.0, values[t])
+            for s in range(group):
+                lower = pairs[device * chunks * group + chunk * group + s]
+                for member in range(2):
+                    wave = lower if member == 0 else waves - 1 - lower
+                    out = jnp.zeros((lats, LANES), jnp.float32)
+                    for f in range(fields):
+                        unit = member * fields + f
+                        spot = unit % 2 * SEATS + s
+                        moved = pltpu.roll(values[unit // 2], (f - spot) * wide % LANES, 1)
+                        out = jnp.where(lane == f, moved, out)
+                    wave_ref[pl.ds(pl.multiple_of(wave * stride, 8), lats), :] = out
             return carry
 
-        lax.fori_loop(0, devices * groups, spread, 0)
+        lax.fori_loop(0, devices * chunks, spread, 0)
 
     total = blocks * rows
     result = jnp.zeros((total, SPAN), jnp.float32)
@@ -225,46 +232,122 @@
                 out_ref[f, l, 0, :, b * SPAN : (b + 1) * SPAN] = piece[start : start + 2]
 
 
-def table_kernel(table_ref, weight_ref, high_ref, low_ref, high_t_ref, low_t_ref, pad_ref):
-    columns = table_ref.shape[2]
-    padded = pad_ref.shape[1]
-    kept = high_t_ref.shape[1]
-    pad_ref[:, padded - LANES :] = jnp.zeros((pad_ref.shape[0], LANES), jnp.float32)
-    pad_ref[:, :columns] = table_ref[0]
-    values = pad_ref[...]
-    high_ref[0], low_ref[0] = halves(values)
-    turned = values.T[:kept] * weight_ref[...]
-    high_t_ref[0], low_t_ref[0] = halves(turned)
-
-
-def legendre_kernel(
-    lowers, come_ref, high_ref, low_ref, high_t_ref, low_t_ref, rate_ref, out_ref, data_ref, damp_ref,
-    *, lev, waves, member
+def exchange_kernel(
+    lowers, sent_ref, table_ref, weight_ref, rate_ref, mine_ref, home_ref,
+    come_ref, back_ref, pad_ref, data_ref, out_sem, in_sem, back_out_sem, back_in_sem, own_sem,
+    *, lev, waves, light, short,
 ):
     slot = pl.program_id(0)
-    devices, fields, _, lats, _ = come_ref.shape
+    chunks, devices, tiles, lats, _ = come_ref.shape
     bands = devices // lev
-    size = 2 * member
-    per_tile = LANES // size
-    pieces = lev * fields
-    tiles = -(-pieces // per_tile)
-    width = tiles * LANES
+    slots = pl.num_programs(0)
+    group = waves // 2 // devices // chunks
+    chunk, spot = slot // group, slot % group
+    band = lax.axis_index("band")
+    me = band * lev + lax.axis_index("lev")
+
+    def message(source, target, send_sem, recv_sem, g, there, where, device, small):
+        part = pl.ds(0, short if small else tiles)
+        return pltpu.make_async_remote_copy(
+            src_ref=source.at[g, there, part],
+            dst_ref=target.at[g, where, part],
+            send_sem=send_sem.at[g, there],
+            recv_sem=recv_sem.at[g, where],
+            device_id=(device // lev, device % lev),
+            device_id_type=pl.DeviceIdType.MESH,
+        )
+
+    def each_other(act, g, small_of):
+        def one(step, carry):
+            other = lax.rem(me + step, devices)
+            small = small_of(other)
+
+            @pl.when(small)
+            def _():
+                act(g, other, True)
+
+            @pl.when(jnp.logical_not(small))
+            def _():
+                act(g, other, False)
+
+            return carry
+
+        lax.fori_loop(1, devices, one, 0)
+
+    def mine_small(other):
+        return band < light
+
+    def their_small(other):
+        return other // lev < light
+
+    def go(g, other, small):
+        message(sent_ref, come_ref, out_sem, in_sem, g, other, me, other, small).start()
+
+    def gone(g, other, small):
+        message(sent_ref, come_ref, out_sem, in_sem, g, other, me, other, small).wait_send()
+
+    def come(g, other, small):
+        message(sent_ref, come_ref, out_sem, in_sem, g, other, other, other, small).wait_recv()
+
+    def back_go(g, other, small):
+        message(back_ref, home_ref, back_out_sem, back_in_sem, g, other, me, other, small).start()
+
+    def back_gone(g, other, small):
+        message(back_ref, home_ref, back_out_sem, back_in_sem, g, other, me, other, small).wait_send()
+
+    def back_come(g, other, small):
+        message(
+            back_ref, home_ref, back_out_sem, back_in_sem, g, other, other, other, small
+        ).wait_recv()
+
+    def own(g):
+        return pltpu.make_async_copy(sent_ref.at[g, me], come_ref.at[g, me], own_sem.at[g])
+
+    def own_back(g):
+        return pltpu.make_async_copy(
+            back_ref.at[g, me], home_ref.at[g, me], own_sem.at[chunks + g]
+        )
+
+    @pl.when(slot == 0)
+    def _():
+        def begin(g, carry):
+            own(g).start()
+            each_other(go, g, mine_small)
+            return carry
+
+        lax.fori_loop(0, chunks, begin, 0)
+        pad_ref[...] = jnp.zeros_like(pad_ref)
+
+    columns = table_ref.shape[1]
+    pad_ref[:columns] = table_ref[0]
+    table_high, table_low = halves(pad_ref[...])
+
+    @pl.when(spot == 0)
+    def _():
+        own(chunk).wait()
+        each_other(come, chunk, their_small)
+
+    arrays = lev * tiles
+    wides = -(-arrays // SEATS)
+    width = wides * LANES
+    member = LANES // (2 * SEATS)
+    seat = iota((lats, LANES), 1) // member % SEATS
+    for b in range(bands):
+        for w in range(wides):
+            value = jnp.zeros((lats, LANES), jnp.float32)
+            for k in range(w * SEATS, min((w + 1) * SEATS, arrays)):
+                if b < light and k % tiles >= short:
+                    continue
+                piece = come_ref[chunk, b * lev + k // tiles, k % tiles]
+                shift = lax.rem((k % SEATS - spot) * member + LANES, LANES)
+                value = jnp.where(seat == k % SEATS, pltpu.roll(piece, shift, 1), value)
+            data_ref[pl.ds(b * lats, lats), w * LANES : (w + 1) * LANES] = value
+    weight = jnp.concatenate([weight_ref[...]] * wides, axis=1)
+    high, low = halves(mirror(data_ref[...]) * weight)
+    first = dot(table_high, jnp.concatenate([high, low], axis=1))
+    analysed = first[:, :width] + (first[:, width:] + dot(table_low, high))
     lower = lowers[slot]
-    spot = lowers[pl.num_programs(0) + slot]
-    lane_piece = iota((lats, LANES), 1) // size
-    for band in range(bands):
-        for t in range(tiles):
-            value = jnp.zeros((lats, LANES), jnp.float32)
-            for k in range(t * per_tile, min((t + 1) * per_tile, pieces)):
-                piece = come_ref[band * lev + k // fields, k % fields, 0]
-                shift = lax.rem((k % per_tile) * size - spot * size + LANES, LANES)
-                value = jnp.where(lane_piece == k % per_tile, pltpu.roll(piece, shift, 1), value)
-            data_ref[pl.ds(band * lats, lats), t * LANES : (t + 1) * LANES] = value
-    high, low = halves(mirror(data_ref[...]))
-    kept = high_t_ref.shape[1]
-    first = dot(high_t_ref[0], jnp.concatenate([high, low], axis=1))
-    analysed = first[:, :width] + (first[:, width:] + dot(low_t_ref[0], high))
-    column = iota((kept, 1), 0)
+    column = iota((pad_ref.shape[0], 1), 0)
     second = column >= waves - lower
     degree = jnp.where(second, column - 1, lower + column)
     order = jnp.where(second, waves - 1 - lower, lower)
@@ -273,27 +356,41 @@
     degree = degree.astype(jnp.float32)
     ratio = degree * (degree + 1.0) * (1.0 / float((waves - 1) * waves))
     square = ratio * ratio
-    lane = iota((1, width), 1)
-    mine = (lane // member % 2) * 2 + lane % 2
-    damped = jnp.where(code == mine, analysed / (1.0 + rate_ref[...] * square), 0.0)
-    damp_ref[:kept] = damped
-    damp_ref[kept:] = jnp.zeros((damp_ref.shape[0] - kept, width), jnp.float32)
-    high, low = halves(damp_ref[...])
-    first = dot(high_ref[0], jnp.concatenate([high, low], axis=1))
-    back = first[:, :width] + (first[:, width:] + dot(low_ref[0], high))
+    damped = jnp.where(code == mine_ref[...], analysed / (1.0 + rate_ref[...] * square), 0.0)
+    high, low = halves(damped)
+    first = dot(table_high.T, jnp.concatenate([high, low], axis=1))
+    back = first[:, :width] + (first[:, width:] + dot(table_low.T, high))
     data_ref[...] = mirror(back)
 
     @pl.when(spot == 0)
     def _():
-        out_ref[...] = jnp.zeros_like(out_ref)
-
-    for band in range(bands):
-        for k in range(pieces):
-            t = k // per_tile
-            piece = data_ref[pl.ds(band * lats, lats), t * LANES : (t + 1) * LANES]
-            shift = lax.rem(spot * size - (k % per_tile) * size + LANES, LANES)
-            target = (band * lev + k // fields, k % fields, 0)
-            out_ref[target] = jnp.where(lane_piece == spot, pltpu.roll(piece, shift, 1), out_ref[target])
+        back_ref[chunk] = jnp.zeros(back_ref.shape[1:], jnp.float32)
+
+    for b in range(bands):
+        for k in range(arrays):
+            if b < light and k % tiles >= short:
+                continue
+            w = k // SEATS
+            piece = data_ref[pl.ds(b * lats, lats), w * LANES : (w + 1) * LANES]
+            shift = lax.rem((spot - k % SEATS) * member + LANES, LANES)
+            target = (chunk, b * lev + k // tiles, k % tiles)
+            back_ref[target] = jnp.where(seat == spot, pltpu.roll(piece, shift, 1), back_ref[target])
+
+    @pl.when(spot == group - 1)
+    def _():
+        own_back(chunk).start()
+        each_other(back_go, chunk, their_small)
+
+    @pl.when(slot == slots - 1)
+    def _():
+        def end(g, carry):
+            own_back(g).wait()
+            each_other(back_come, g, mine_small)
+            each_other(gone, g, mine_small)
+            each_other(back_gone, g, their_small)
+            return carry
+
+        lax.fori_loop(0, chunks, end, 0)
 
 
 def body(field_grid, increment, points, weights, pair_slot, legendre, strength):
@@ -304,18 +401,23 @@
     waves = length // 2
     slots, half, columns = legendre.shape
     member = 4 * local
+    assert member * 2 * SEATS == LANES
     pair_count = waves // 2
     ranks = lax.iota(jnp.int32, pair_count)
     pairs = jnp.sum(jnp.where(pair_slot[None, :] == ranks[:, None], ranks[None, :], 0), axis=1)
-    group = max(
-        g for g in range(2, 2 * slots + 1, 2) if 2 * slots % g == 0 and g * member <= LANES
-    )
-    groups = 2 * slots // group
+    group = max(g for g in range(1, SEATS + 1) if slots % g == 0)
+    chunks = slots // group
+    tiles = fields
+    short = (fields + 1) // 2
+    most = [
+        min(length, 48 + (length - 16) * (lats * (b + 1) - 1) // (half - 1)) for b in range(bands)
+    ]
+    light = sum((cells - 1) // 2 < pair_count for cells in most)
     stride = -(-lats // 8) * 8
     blocks = length // SPAN
     rows = fields * local * 2
     grid_block = pl.BlockSpec((fields, local, 1, 2, length), lambda j, *_: (0, 0, j, 0, 0))
-    buffer = (devices, fields, groups, lats, LANES)
+    buffer = (chunks, devices, tiles, lats, LANES)
     whole_block = pl.BlockSpec(buffer, lambda j, *_: (0, 0, 0, 0, 0))
     waved = pltpu.VMEM((waves * stride, LANES), jnp.float32)
     flops = lats * 6 * blocks * rows * SPAN * length
@@ -336,63 +438,62 @@
         ),
         cost_estimate=pl.CostEstimate(flops=flops, bytes_accessed=0, transcendentals=0),
     )(points, pairs, field_grid, increment)
-    arrived = lax.all_to_all(sent, ("band", "lev"), split_axis=0, concat_axis=0, tiled=True)
-
+
+    arrays = lev * tiles
+    width = -(-arrays // SEATS) * LANES
     padded = -(-columns // LANES) * LANES
-    kept = -(-columns // 16) * 16
-    plain = pl.BlockSpec((1, half, padded), lambda s, *_: (s, 0, 0))
-    turned = pl.BlockSpec((1, kept, half), lambda s, *_: (s, 0, 0))
-    tables = pl.pallas_call(
-        table_kernel,
-        out_shape=[jax.ShapeDtypeStruct((slots, half, padded), jnp.bfloat16)] * 2
-        + [jax.ShapeDtypeStruct((slots, kept, half), jnp.bfloat16)] * 2,
-        grid=(slots,),
-        in_specs=[
-            pl.BlockSpec((1, half, columns), lambda s: (s, 0, 0)),
-            pl.BlockSpec((1, half), lambda s: (0, 0)),
-        ],
-        out_specs=[plain, plain, turned, turned],
-        scratch_shapes=[pltpu.VMEM((half, padded), jnp.float32)],
-        cost_estimate=pl.CostEstimate(
-            flops=slots * 4 * half * padded * 256, bytes_accessed=0, transcendentals=0
-        ),
-    )(legendre, weights[None, :])
-
-    size = 2 * member
-    per_tile = LANES // size
-    tiles = -(-lev * fields // per_tile)
-    width = tiles * LANES
-    rate = jnp.moveaxis(strength.reshape(fields, lev, local), 1, 0)
-    rate = jnp.broadcast_to(rate[:, :, None, :, None], (lev, fields, 4, local, 2)).reshape(1, -1)
-    rate = jnp.pad(rate, ((0, 0), (0, width - rate.shape[1])))
+    lane = np.arange(width)
+    seat = lane % LANES // member
+    array = lane // LANES * SEATS + seat % SEATS
+    unit = array % tiles * 2 + seat // SEATS
+    real = array < arrays
+    mine = np.where(real, unit // fields * 2 + lane % 2, -2)
+    level = array // tiles * local + lane // 2 % local
+    rank = np.where(real, unit % fields * lev * local + level, 0)
+    choice = jnp.asarray(np.arange(fields * lev * local)[:, None] == rank[None, :], jnp.float32)
+    rate = jnp.sum(choice * strength.reshape(-1, 1), axis=0, keepdims=True)
     own = lax.dynamic_slice_in_dim(pairs, lax.axis_index(("band", "lev")) * slots, slots)
-    per_group = group // 2
-    lowers = jnp.concatenate([own, lax.iota(jnp.int32, slots) % per_group])
-    mail = pl.BlockSpec((devices, fields, 1, lats, LANES), lambda s, *_: (0, 0, s // per_group, 0, 0))
-    returned = pl.pallas_call(
-        functools.partial(legendre_kernel, lev=lev, waves=waves, member=member),
+    home = pl.pallas_call(
+        functools.partial(exchange_kernel, lev=lev, waves=waves, light=light, short=short),
         out_shape=jax.ShapeDtypeStruct(buffer, jnp.float32),
         grid_spec=pltpu.PrefetchScalarGridSpec(
             num_scalar_prefetch=1,
             grid=(slots,),
             in_specs=[
-                mail, plain, plain, turned, turned,
+                pl.BlockSpec(memory_space=pl.ANY),
+                pl.BlockSpec((1, columns, half), lambda s, *_: (s, 0, 0)),
+                pl.BlockSpec((half, LANES), lambda s, *_: (0, 0)),
+                pl.BlockSpec((1, width), lambda s, *_: (0, 0)),
                 pl.BlockSpec((1, width), lambda s, *_: (0, 0)),
             ],
-            out_specs=mail,
+            out_specs=pl.BlockSpec(memory_space=pl.ANY),
             scratch_shapes=[
+                pltpu.VMEM(buffer, jnp.float32),
+                pltpu.VMEM(buffer, jnp.float32),
+                pltpu.VMEM((padded, half), jnp.float32),
                 pltpu.VMEM((half, width), jnp.float32),
-                pltpu.VMEM((padded, width), jnp.float32),
+                pltpu.SemaphoreType.DMA((chunks, devices)),
+                pltpu.SemaphoreType.DMA((chunks, devices)),
+                pltpu.SemaphoreType.DMA((chunks, devices)),
+                pltpu.SemaphoreType.DMA((chunks, devices)),
+                pltpu.SemaphoreType.DMA((2 * chunks,)),
             ],
         ),
+        compiler_params=pltpu.CompilerParams(has_side_effects=True),
         cost_estimate=pl.CostEstimate(
             flops=slots * 12 * half * padded * width, bytes_accessed=0, transcendentals=0
         ),
-    )(lowers, arrived, *tables, rate)
-    home = lax.all_to_all(returned, ("band", "lev"), split_axis=0, concat_axis=0, tiled=True)
+    )(
+        own,
+        sent,
+        jnp.swapaxes(legendre, 1, 2),
+        jnp.broadcast_to(weights[:, None], (half, LANES)),
+        rate,
+        jnp.asarray(mine[None, :], jnp.int32),
+    )
 
     return pl.pallas_call(
-        functools.partial(inverse_kernel, stride=stride),
+        functools.partial(inverse_kernel, stride=stride, light=light, short=short),
         out_shape=jax.ShapeDtypeStruct(field_grid.shape, jnp.float32),
         grid_spec=pltpu.PrefetchScalarGridSpec(
             num_scalar_prefetch=2,

time: 304 us -> 231 us (0.76); the launches traced: 299 us -> 230 us
  blocking collectives: 83.7 us -> 0 us
  Pallas kernels: 147 us -> 225 us
  waiting for transfers between devices: 38 us -> 0 us
  local copies, waits for them, and re-layouts: 21.7 us -> 2.78 us
  starting transfers between devices: 6.14 us -> 0 us
    all_to_all x1 -> x0, blocking collectives: 83.7 us -> none  [body(): lax.all_to_all(returned, ('band', 'lev'), split_axis=0, concat_axis=0, ti...]
    pallas_call x3 -> x2, Pallas kernels: 106 us -> 185 us  [the longest x1 147 us: body(): pl.pallas_call(functools.partial(exchange_kernel, lev=lev, waves=waves, l...]
    all_to_all x1 -> x0, waiting for transfers between devices: 38 us -> none  [body(): lax.all_to_all(sent, ('band', 'lev'), split_axis=0, concat_axis=0, tiled=...]
    unnamed x7 -> x2, local copies, waits for them, and re-layouts: 18.1 us -> 0.01 us
    all_to_all x1 -> x0, starting transfers between devices: 6.14 us -> none  [body(): lax.all_to_all(sent, ('band', 'lev'), split_axis=0, concat_axis=0, tiled=...]
  transfers between devices with their start and end apart: 1 -> 0, of which waited for: 1 -> 0; matrix products, arithmetic and copies ran while one was open for 7% -> 0% of each run, Pallas kernels for 6% -> 0%
where the time goes in v1:
time: 231 us; the launch traced here: 230 us
  Pallas kernels  225 us (97%)
  local copies, waits for them, and re-layouts  2.78 us (1%)
    pallas_call x1, Pallas kernels, body(): pl.pallas_call(functools.partial(exchange_kernel, lev=lev, waves=waves, l...  147 us
    pallas_call x1, Pallas kernels, body(): pl.pallas_call(functools.partial(forward_kernel, stride=stride), out_shap...  40.5 us
    pallas_call x1, Pallas kernels, body(): pl.pallas_call(functools.partial(inverse_kernel, stride=stride, light=lig...  37.5 us

profile of v1, /device:TPU:27, one launch (start us, length us, event | category | flops | bytes accessed | tf_op | source)
XLA Modules:
  0.0 230.4 jit_solution(11436275328678071091)
XLA Ops:
  0.0 0.8 mul.18
  0.8 1.4 multiply_reduce_fusion
  2.2 0.8 select_reduce_fusion.pairs
  3.0 0.0 copy-start
  3.0 0.6 dynamic_slice.3.lowers
  3.6 1.5 broadcast_in_dim.26.weight_ref
  5.0 0.0 copy-done
  5.0 40.5 %shard_map.91.sent_ref = f32[3,32,3,24,128]{4,3,2,1,0:T(8,128)} custom-call(s32[24]{0:T(128)} %counts.3, s32[384]{0:T(512)} %copy-done, f32[3,4,24,2,1536]{4,3,2,1,0:T(2,128)} %field_ref.1, f32[3,4,24,2,1536]{4,3,2,1,0:T(2,128)} %more_ref.1), custom_call_target="tpu_custom_call" | custom-call | flops 8153726976 | tf_op jit(solution)/shard_map/pallas_call | solution.py:424
  45.6 147.3 %shard_map.92.come_ref = f32[3,32,3,24,128]{4,3,2,1,0:T(8,128)} custom-call(s32[12]{0:T(128)} %dynamic_slice.3.lowers, f32[3,32,3,24,128]{4,3,2,1,0:T(8,128)} %shard_map.91.sent_ref, f32[12,769,384]{2,1,0:T(8,128)} %bitcast.3, f32[384,128]{1,0:T(8,128)} %broadcast_in_dim.26.weight_ref, f32[1,256]{1,0:T(1,128)} %bitcast.2, s32[1,256]{1,0:T(1,128)} %constant.23.clone.mine_ref), custom_call_target="tpu_custom_call" | custom-call | flops 12683575296 | tf_op jit(solution)/shard_map/pallas_call | solution.py:456
  192.9 37.5 %shard_map.93 = f32[3,4,24,2,1536]{4,3,2,1,0:T(2,128)} custom-call(s32[24]{0:T(128)} %counts.3, s32[384]{0:T(512)} %copy-done, f32[3,32,3,24,128]{4,3,2,1,0:T(8,128)} %shard_map.92.come_ref), custom_call_target="tpu_custom_call" | custom-call | flops 8153726976 | tf_op jit(solution)/shard_map/pallas_call | solution.py:495
Async XLA Ops:
  3.0 2.0 copy-start

commit v2 on v1

--- a/solution.py
+++ b/solution.py
@@ -1,5 +1,4 @@
 import functools
-import math
 
 import jax
 import jax.numpy as jnp
@@ -13,8 +12,12 @@
 SPAN = 256
 FINE = 16
 SEATS = 4
-SINE = [(-1) ** k * math.pi ** (2 * k + 1) / math.factorial(2 * k + 1) for k in range(6)]
-COSINE = [(-1) ** k * math.pi ** (2 * k) / math.factorial(2 * k) for k in range(7)]
+UNROLL = 4
+EACH = 4
+SUB = 2
+HALF_SPAN = SPAN // 2
+SINE = [3.14159264, -5.16771008, 2.55007739, -0.59829041, 0.07765591]
+COSINE = [0.99999995, -4.9347928, 4.05841079, -1.33187297, 0.21968242]
 
 
 def halves(values):
@@ -24,6 +27,10 @@
 
 def iota(shape, dim):
     return lax.broadcasted_iota(jnp.int32, shape, dim)
+
+
+def seat_of(field):
+    return field % 2 * SEATS + field // 2 * 2
 
 
 def turn(product, count, inverse):
@@ -45,6 +52,11 @@
     )
 
 
+def reverse(values):
+    back = values.shape[1] - 1 - iota(values.shape, 1)
+    return jnp.take_along_axis(values, back, axis=1, mode="promise_in_bounds")
+
+
 def mirror(values):
     lane = iota(values.shape, 1)
     width = values.shape[1]
@@ -56,7 +68,8 @@
 
 
 def forward_kernel(
-    counts, pairs, field_ref, more_ref, out_ref, row_ref, high_ref, low_ref, wave_ref, *, stride
+    counts, pairs, weights, field_ref, more_ref, out_ref, row_ref, high_ref, low_ref, wave_ref,
+    *, stride,
 ):
     fields, local, _, _, length = field_ref.shape
     chunks, devices, tiles, lats, _ = out_ref.shape
@@ -66,58 +79,74 @@
     wide = 2 * each
     group = waves // 2 // devices // chunks
     blocks = length // SPAN
-    lat = pl.program_id(0)
-    count = counts[lat]
-    real = count.astype(jnp.float32)
-    inverse = 1.0 / jnp.full((1, 1), real, jnp.float32)
-    for f in range(fields):
-        for l in range(local):
-            row_ref[pl.ds((f * local + l) * 2, 2), :] = field_ref[f, l, 0] + more_ref[f, l, 0]
-    pieces = []
-    for b in range(blocks):
-        piece = row_ref[:, b * SPAN : (b + 1) * SPAN]
-        place = b * SPAN + iota(piece.shape, 1)
-        pieces.append(jnp.where(place < count, piece, 0.0))
-    high, low = halves(jnp.concatenate(pieces, axis=0))
-    both = jnp.concatenate([high, low], axis=0)
-    total = blocks * rows
-    for q in range(waves // SPAN):
-        order = q * SPAN + iota((1, SPAN), 1)
-        order = order.astype(jnp.float32)
-        steps = iota((FINE, SPAN), 0).astype(jnp.float32)
-        fine_cos, fine_sin = turn(steps * order, real, inverse)
-        coarse_cos, coarse_sin = turn(FINE * steps * order, real, inverse)
-        block_cos, block_sin = turn(SPAN * steps[:8] * order, real, inverse)
-        for i in range(SPAN // FINE):
-            cosine, sine = coarse_cos[i : i + 1], coarse_sin[i : i + 1]
-            place = pl.ds(i * FINE, FINE)
-            top, rest = halves(cosine * fine_cos - sine * fine_sin)
-            high_ref[q, place, :SPAN] = top
-            low_ref[q, place, :SPAN] = rest
-            top, rest = halves(sine * fine_cos + cosine * fine_sin)
-            high_ref[q, place, SPAN:] = top
-            low_ref[q, place, SPAN:] = rest
-        first = dot(both, high_ref[q])
-        product = first[:total] + (first[total:] + dot(high, low_ref[q]))
-        real_part = jnp.zeros((rows, SPAN), jnp.float32)
-        imaginary = jnp.zeros((rows, SPAN), jnp.float32)
+    each_step = field_ref.shape[2]
+
+    def one(sub, carry):
+        lat = pl.program_id(0) * each_step + sub
+        count = counts[lat]
+        real = 2.0 * count.astype(jnp.float32)
+        inverse = 1.0 / jnp.full((1, 1), real, jnp.float32)
+        for f in range(fields):
+            for l in range(local):
+                row_ref[pl.ds((f * local + l) * 2, 2), :] = field_ref[f, l, sub] + more_ref[f, l, sub]
+        evens, odds = [], []
         for b in range(blocks):
-            in_cos = product[b * rows : (b + 1) * rows, :SPAN]
-            in_sin = product[b * rows : (b + 1) * rows, SPAN:]
-            cosine, sine = block_cos[b : b + 1], block_sin[b : b + 1]
-            real_part += cosine * in_cos - sine * in_sin
-            imaginary -= sine * in_cos + cosine * in_sin
-        live = order.astype(jnp.int32) <= (count - 1) // 2
-        scale = jnp.where(live, inverse, 0.0)
-        real_part, imaginary = real_part * scale, imaginary * scale
-        parts = []
-        for f in range(fields):
-            parts += [real_part[f * each : (f + 1) * each], imaginary[f * each : (f + 1) * each]]
-        parts.append(jnp.zeros((LANES - fields * wide, SPAN), jnp.float32))
-        turned = jnp.concatenate(parts, axis=0).T
-        wave_ref[pl.ds(q * SPAN * stride + lat, SPAN, stride=stride), :] = turned
-
-    @pl.when(lat == pl.num_programs(0) - 1)
+            piece = row_ref[:, b * SPAN : (b + 1) * SPAN]
+            place = b * SPAN + iota(piece.shape, 1)
+            piece = jnp.where(place < count, piece, 0.0)
+            right, left = piece[:, HALF_SPAN:], reverse(piece[:, :HALF_SPAN])
+            evens.append(right + left)
+            odds.append(right - left)
+        even, even_low = halves(jnp.concatenate(evens, axis=0))
+        odd, odd_low = halves(jnp.concatenate(odds, axis=0))
+        evens = jnp.concatenate([even, even_low], axis=0)
+        odds = jnp.concatenate([odd, odd_low], axis=0)
+        total = blocks * rows
+        weight = weights[lax.axis_index("band") * lats + lat]
+        for q in range(waves // SPAN):
+            order = q * SPAN + iota((1, SPAN), 1)
+            order = order.astype(jnp.float32)
+            steps = iota((FINE, SPAN), 0).astype(jnp.float32)
+            fine_cos, fine_sin = turn((2.0 * steps + 1.0) * order, real, inverse)
+            steps = steps[:8]
+            coarse_cos, coarse_sin = turn(2 * FINE * steps * order, real, inverse)
+            block_cos, block_sin = turn((2 * SPAN * steps + (SPAN - 1)) * order, real, inverse)
+            for i in range(HALF_SPAN // FINE):
+                cosine, sine = coarse_cos[i : i + 1], coarse_sin[i : i + 1]
+                place = pl.ds(i * FINE, FINE)
+                top, rest = halves(cosine * fine_cos - sine * fine_sin)
+                high_ref[q, place, :SPAN] = top
+                low_ref[q, place, :SPAN] = rest
+                top, rest = halves(sine * fine_cos + cosine * fine_sin)
+                high_ref[q, place, SPAN:] = top
+                low_ref[q, place, SPAN:] = rest
+            first = dot(evens, high_ref[q, :, :SPAN])
+            with_cos = first[:total] + (first[total:] + dot(even, low_ref[q, :, :SPAN]))
+            first = dot(odds, high_ref[q, :, SPAN:])
+            with_sin = first[:total] + (first[total:] + dot(odd, low_ref[q, :, SPAN:]))
+            real_part = jnp.zeros((rows, SPAN), jnp.float32)
+            imaginary = jnp.zeros((rows, SPAN), jnp.float32)
+            for b in range(blocks):
+                in_cos = with_cos[b * rows : (b + 1) * rows]
+                in_sin = with_sin[b * rows : (b + 1) * rows]
+                cosine, sine = block_cos[b : b + 1], block_sin[b : b + 1]
+                real_part += cosine * in_cos - sine * in_sin
+                imaginary -= sine * in_cos + cosine * in_sin
+            live = order.astype(jnp.int32) <= (count - 1) // 2
+            scale = jnp.where(live, 2.0 * weight * inverse, 0.0)
+            real_part, imaginary = real_part * scale, imaginary * scale
+            parts = [jnp.zeros((wide, SPAN), jnp.float32)] * (LANES // wide)
+            for f in range(fields):
+                parts[seat_of(f)] = jnp.concatenate(
+                    [real_part[f * each : (f + 1) * each], imaginary[f * each : (f + 1) * each]], axis=0
+                )
+            turned = jnp.concatenate(parts, axis=0).T
+            wave_ref[pl.ds(q * SPAN * stride + lat, SPAN, stride=stride), :] = turned
+        return carry
+
+    lax.fori_loop(0, each_step, one, 0, unroll=SUB)
+
+    @pl.when(pl.program_id(0) == pl.num_programs(0) - 1)
     def _():
         lane = iota((lats, LANES), 1) // wide
 
@@ -128,17 +157,20 @@
                 lower = pairs[device * chunks * group + chunk * group + s]
                 for member in range(2):
                     wave = lower if member == 0 else waves - 1 - lower
-                    value = wave_ref[pl.ds(pl.multiple_of(wave * stride, 8), lats), :]
+                    value = wave_ref[pl.ds(wave * stride, lats), :]
+                    moved = {}
                     for f in range(fields):
                         unit = member * fields + f
                         spot = unit % 2 * SEATS + s
-                        moved = pltpu.roll(value, (spot - f) * wide % LANES, 1)
-                        outs[unit // 2] = jnp.where(lane == spot, moved, outs[unit // 2])
+                        step = (spot - seat_of(f)) * wide % LANES
+                        if step not in moved:
+                            moved[step] = pltpu.roll(value, step, 1)
+                        outs[unit // 2] = jnp.where(lane == spot, moved[step], outs[unit // 2])
             for t in range(tiles):
                 out_ref[chunk, device, t] = outs[t]
             return carry
 
-        lax.fori_loop(0, devices * chunks, assemble, 0)
+        lax.fori_loop(0, devices * chunks, assemble, 0, unroll=UNROLL)
 
 
 def inverse_kernel(
@@ -152,12 +184,9 @@
     wide = 2 * each
     group = waves // 2 // devices // chunks
     blocks = length // SPAN
-    lat = pl.program_id(0)
-    count = counts[lat]
-    real = count.astype(jnp.float32)
-    inverse = 1.0 / jnp.full((1, 1), real, jnp.float32)
-
-    @pl.when(lat == 0)
+    each_step = out_ref.shape[2]
+
+    @pl.when(pl.program_id(0) == 0)
     def _():
         lane = iota((lats, LANES), 1) // wide
         small = lax.axis_index("band") < light
@@ -172,68 +201,84 @@
                 for member in range(2):
                     wave = lower if member == 0 else waves - 1 - lower
                     out = jnp.zeros((lats, LANES), jnp.float32)
+                    moved = {}
                     for f in range(fields):
                         unit = member * fields + f
                         spot = unit % 2 * SEATS + s
-                        moved = pltpu.roll(values[unit // 2], (f - spot) * wide % LANES, 1)
-                        out = jnp.where(lane == f, moved, out)
-                    wave_ref[pl.ds(pl.multiple_of(wave * stride, 8), lats), :] = out
+                        step = (seat_of(f) - spot) * wide % LANES
+                        if (unit // 2, step) not in moved:
+                            moved[unit // 2, step] = pltpu.roll(values[unit // 2], step, 1)
+                        out = jnp.where(lane == seat_of(f), moved[unit // 2, step], out)
+                    wave_ref[pl.ds(wave * stride, lats), :] = out
             return carry
 
-        lax.fori_loop(0, devices * chunks, spread, 0)
-
-    total = blocks * rows
-    result = jnp.zeros((total, SPAN), jnp.float32)
-    place = iota((1, SPAN), 1).astype(jnp.float32)
-    steps = iota((FINE, SPAN), 0).astype(jnp.float32)
-    fine_cos, fine_sin = turn(steps * place, real, inverse)
-    for q in range(waves // SPAN):
-        start = float(q * SPAN)
-        coarse_cos, coarse_sin = turn((start + FINE * steps) * place, real, inverse)
-        order = start + place
-        block_cos, block_sin = turn(SPAN * steps[:8] * order, real, inverse)
-        for i in range(SPAN // FINE):
-            cosine, sine = coarse_cos[i : i + 1], coarse_sin[i : i + 1]
-            top, rest = halves(cosine * fine_cos - sine * fine_sin)
-            high_ref[q, i * FINE : (i + 1) * FINE] = top
-            low_ref[q, i * FINE : (i + 1) * FINE] = rest
-            top, rest = halves(-(sine * fine_cos + cosine * fine_sin))
-            high_ref[q, SPAN + i * FINE : SPAN + (i + 1) * FINE] = top
-            low_ref[q, SPAN + i * FINE : SPAN + (i + 1) * FINE] = rest
-        turned = wave_ref[pl.ds(q * SPAN * stride + lat, SPAN, stride=stride), :].T
-        real_part = jnp.concatenate(
-            [turned[f * wide : f * wide + each] for f in range(fields)], axis=0
-        )
-        imaginary = jnp.concatenate(
-            [turned[f * wide + each : (f + 1) * wide] for f in range(fields)], axis=0
-        )
-        wave = order.astype(jnp.int32)
-        double = jnp.where(wave == 0, 1.0, 2.0)
-        double = jnp.where(wave <= (count - 1) // 2, double, 0.0)
-        block_cos, block_sin = block_cos * double, block_sin * double
-        shifted = []
+        lax.fori_loop(0, devices * chunks, spread, 0, unroll=UNROLL)
+
+    def one(sub, carry):
+        lat = pl.program_id(0) * each_step + sub
+        count = counts[lat]
+        real = 2.0 * count.astype(jnp.float32)
+        inverse = 1.0 / jnp.full((1, 1), real, jnp.float32)
+        total = blocks * rows
+        with_cos = jnp.zeros((total, HALF_SPAN), jnp.float32)
+        with_sin = jnp.zeros((total, HALF_SPAN), jnp.float32)
+        place = 2.0 * iota((1, HALF_SPAN), 1).astype(jnp.float32) + 1.0
+        steps = iota((FINE, HALF_SPAN), 0).astype(jnp.float32)
+        fine_cos, fine_sin = turn(steps * place, real, inverse)
+        for q in range(waves // SPAN):
+            start = q * SPAN
+            coarse_cos, coarse_sin = turn((start + FINE * steps) * place, real, inverse)
+            order = start + iota((1, SPAN), 1).astype(jnp.float32)
+            rank = iota((8, SPAN), 0).astype(jnp.float32)
+            block_cos, block_sin = turn((2 * SPAN * rank + (SPAN - 1)) * order, real, inverse)
+            for i in range(SPAN // FINE):
+                cosine, sine = coarse_cos[i : i + 1], coarse_sin[i : i + 1]
+                part = pl.ds(i * FINE, FINE)
+                top, rest = halves(cosine * fine_cos - sine * fine_sin)
+                high_ref[q, 0, part] = top
+                low_ref[q, 0, part] = rest
+                top, rest = halves(sine * fine_cos + cosine * fine_sin)
+                high_ref[q, 1, part] = top
+                low_ref[q, 1, part] = rest
+            turned = wave_ref[pl.ds(q * SPAN * stride + lat, SPAN, stride=stride), :].T
+            real_part = jnp.concatenate(
+                [turned[seat_of(f) * wide :][:each] for f in range(fields)], axis=0
+            )
+            imaginary = jnp.concatenate(
+                [turned[seat_of(f) * wide + each :][:each] for f in range(fields)], axis=0
+            )
+            wave = order.astype(jnp.int32)
+            double = jnp.where(wave == 0, 1.0, 2.0)
+            double = jnp.where(wave <= (count - 1) // 2, double, 0.0)
+            block_cos, block_sin = block_cos * double, block_sin * double
+            evens, odds = [], []
+            for b in range(blocks):
+                cosine, sine = block_cos[b : b + 1], block_sin[b : b + 1]
+                evens.append(real_part * cosine - imaginary * sine)
+                odds.append(real_part * sine + imaginary * cosine)
+            even, low = halves(jnp.concatenate(evens, axis=0))
+            first = dot(jnp.concatenate([even, low], axis=0), high_ref[q, 0])
+            with_cos += first[:total] + (first[total:] + dot(even, low_ref[q, 0]))
+            odd, low = halves(jnp.concatenate(odds, axis=0))
+            first = dot(jnp.concatenate([odd, low], axis=0), high_ref[q, 1])
+            with_sin += first[:total] + (first[total:] + dot(odd, low_ref[q, 1]))
+        right, left = with_cos - with_sin, reverse(with_cos + with_sin)
         for b in range(blocks):
-            cosine, sine = block_cos[b : b + 1], block_sin[b : b + 1]
-            shifted.append(
-                jnp.concatenate(
-                    [real_part * cosine - imaginary * sine, real_part * sine + imaginary * cosine],
-                    axis=1,
-                )
-            )
-        high, low = halves(jnp.concatenate(shifted, axis=0))
-        first = dot(jnp.concatenate([high, low], axis=0), high_ref[q])
-        result += first[:total] + (first[total:] + dot(high, low_ref[q]))
-    for b in range(blocks):
-        live = b * SPAN + iota((rows, SPAN), 1) < count
-        piece = jnp.where(live, result[b * rows : (b + 1) * rows], 0.0)
-        for f in range(fields):
-            for l in range(local):
-                start = (f * local + l) * 2
-                out_ref[f, l, 0, :, b * SPAN : (b + 1) * SPAN] = piece[start : start + 2]
+            for part, side in ((0, left), (1, right)):
+                start = b * SPAN + part * HALF_SPAN
+                live = start + iota((rows, HALF_SPAN), 1) < count
+                piece = jnp.where(live, side[b * rows : (b + 1) * rows], 0.0)
+                for f in range(fields):
+                    for l in range(local):
+                        row = (f * local + l) * 2
+                        out_ref[f, l, sub, :, start : start + HALF_SPAN] = piece[row : row + 2]
+        return carry
+
+    lax.fori_loop(0, each_step, one, 0, unroll=SUB)
 
 
 def exchange_kernel(
-    lowers, sent_ref, table_ref, weight_ref, rate_ref, mine_ref, home_ref,
+    lowers, rates, sent_ref, table_ref, rank_ref, mine_ref, home_ref,
     come_ref, back_ref, pad_ref, data_ref, out_sem, in_sem, back_out_sem, back_in_sem, own_sem,
     *, lev, waves, light, short,
 ):
@@ -342,8 +387,7 @@
                 shift = lax.rem((k % SEATS - spot) * member + LANES, LANES)
                 value = jnp.where(seat == k % SEATS, pltpu.roll(piece, shift, 1), value)
             data_ref[pl.ds(b * lats, lats), w * LANES : (w + 1) * LANES] = value
-    weight = jnp.concatenate([weight_ref[...]] * wides, axis=1)
-    high, low = halves(mirror(data_ref[...]) * weight)
+    high, low = halves(mirror(data_ref[...]))
     first = dot(table_high, jnp.concatenate([high, low], axis=1))
     analysed = first[:, :width] + (first[:, width:] + dot(table_low, high))
     lower = lowers[slot]
@@ -356,7 +400,10 @@
     degree = degree.astype(jnp.float32)
     ratio = degree * (degree + 1.0) * (1.0 / float((waves - 1) * waves))
     square = ratio * ratio
-    damped = jnp.where(code == mine_ref[...], analysed / (1.0 + rate_ref[...] * square), 0.0)
+    rate = jnp.zeros(rank_ref.shape, jnp.float32)
+    for r in range(rates.shape[0]):
+        rate = jnp.where(rank_ref[...] == r, rates[r], rate)
+    damped = jnp.where(code == mine_ref[...], analysed / (1.0 + rate * square), 0.0)
     high, low = halves(damped)
     first = dot(table_high.T, jnp.concatenate([high, low], axis=1))
     back = first[:, :width] + (first[:, width:] + dot(table_low.T, high))
@@ -413,10 +460,11 @@
         min(length, 48 + (length - 16) * (lats * (b + 1) - 1) // (half - 1)) for b in range(bands)
     ]
     light = sum((cells - 1) // 2 < pair_count for cells in most)
-    stride = -(-lats // 8) * 8
+    stride = lats + 1 - lats % 2
     blocks = length // SPAN
     rows = fields * local * 2
-    grid_block = pl.BlockSpec((fields, local, 1, 2, length), lambda j, *_: (0, 0, j, 0, 0))
+    each_step = max(g for g in range(1, EACH + 1) if lats % g == 0)
+    grid_block = pl.BlockSpec((fields, local, each_step, 2, length), lambda j, *_: (0, 0, j, 0, 0))
     buffer = (chunks, devices, tiles, lats, LANES)
     whole_block = pl.BlockSpec(buffer, lambda j, *_: (0, 0, 0, 0, 0))
     waved = pltpu.VMEM((waves * stride, LANES), jnp.float32)
@@ -425,19 +473,19 @@
         functools.partial(forward_kernel, stride=stride),
         out_shape=jax.ShapeDtypeStruct(buffer, jnp.float32),
         grid_spec=pltpu.PrefetchScalarGridSpec(
-            num_scalar_prefetch=2,
-            grid=(lats,),
+            num_scalar_prefetch=3,
+            grid=(lats // each_step,),
             in_specs=[grid_block, grid_block],
             out_specs=whole_block,
             scratch_shapes=[
                 pltpu.VMEM((rows, length), jnp.float32),
-                pltpu.VMEM((waves // SPAN, SPAN, 2 * SPAN), jnp.bfloat16),
-                pltpu.VMEM((waves // SPAN, SPAN, 2 * SPAN), jnp.bfloat16),
+                pltpu.VMEM((waves // SPAN, HALF_SPAN, 2 * SPAN), jnp.bfloat16),
+                pltpu.VMEM((waves // SPAN, HALF_SPAN, 2 * SPAN), jnp.bfloat16),
                 waved,
             ],
         ),
         cost_estimate=pl.CostEstimate(flops=flops, bytes_accessed=0, transcendentals=0),
-    )(points, pairs, field_grid, increment)
+    )(points, pairs, weights, field_grid, increment)
 
     arrays = lev * tiles
     width = -(-arrays // SEATS) * LANES
@@ -450,19 +498,16 @@
     mine = np.where(real, unit // fields * 2 + lane % 2, -2)
     level = array // tiles * local + lane // 2 % local
     rank = np.where(real, unit % fields * lev * local + level, 0)
-    choice = jnp.asarray(np.arange(fields * lev * local)[:, None] == rank[None, :], jnp.float32)
-    rate = jnp.sum(choice * strength.reshape(-1, 1), axis=0, keepdims=True)
     own = lax.dynamic_slice_in_dim(pairs, lax.axis_index(("band", "lev")) * slots, slots)
     home = pl.pallas_call(
         functools.partial(exchange_kernel, lev=lev, waves=waves, light=light, short=short),
         out_shape=jax.ShapeDtypeStruct(buffer, jnp.float32),
         grid_spec=pltpu.PrefetchScalarGridSpec(
-            num_scalar_prefetch=1,
+            num_scalar_prefetch=2,
             grid=(slots,),
             in_specs=[
                 pl.BlockSpec(memory_space=pl.ANY),
                 pl.BlockSpec((1, columns, half), lambda s, *_: (s, 0, 0)),
-                pl.BlockSpec((half, LANES), lambda s, *_: (0, 0)),
                 pl.BlockSpec((1, width), lambda s, *_: (0, 0)),
                 pl.BlockSpec((1, width), lambda s, *_: (0, 0)),
             ],
@@ -485,10 +530,10 @@
         ),
     )(
         own,
+        strength.reshape(-1),
         sent,
         jnp.swapaxes(legendre, 1, 2),
-        jnp.broadcast_to(weights[:, None], (half, LANES)),
-        rate,
+        jnp.asarray(rank[None, :], jnp.int32),
         jnp.asarray(mine[None, :], jnp.int32),
     )
 
@@ -497,12 +542,12 @@
         out_shape=jax.ShapeDtypeStruct(field_grid.shape, jnp.float32),
         grid_spec=pltpu.PrefetchScalarGridSpec(
             num_scalar_prefetch=2,
-            grid=(lats,),
+            grid=(lats // each_step,),
             in_specs=[whole_block],
             out_specs=grid_block,
             scratch_shapes=[
-                pltpu.VMEM((waves // SPAN, 2 * SPAN, SPAN), jnp.bfloat16),
-                pltpu.VMEM((waves // SPAN, 2 * SPAN, SPAN), jnp.bfloat16),
+                pltpu.VMEM((waves // SPAN, 2, SPAN, HALF_SPAN), jnp.bfloat16),
+                pltpu.VMEM((waves // SPAN, 2, SPAN, HALF_SPAN), jnp.bfloat16),
                 waved,
             ],
         ),

time: 231 us -> 202 us (0.87)
  Pallas kernels: 225 us -> 199 us
    pallas_call x1, Pallas kernels: 40.5 us -> 24.6 us  [body(): pl.pallas_call(functools.partial(forward_kernel, stride=stride), out_shap...]
    pallas_call x1, Pallas kernels: 37.5 us -> 27.3 us  [body(): pl.pallas_call(functools.partial(inverse_kernel, stride=stride, light=lig...]
where the time goes in v2:
time: 202 us
  Pallas kernels  199 us (99%)
    pallas_call x1, Pallas kernels, body(): pl.pallas_call(functools.partial(exchange_kernel, lev=lev, waves=waves, l...  147 us
    pallas_call x1, Pallas kernels, body(): pl.pallas_call(functools.partial(inverse_kernel, stride=stride, light=lig...  27.3 us
    pallas_call x1, Pallas kernels, body(): pl.pallas_call(functools.partial(forward_kernel, stride=stride), out_shap...  24.6 us

profile of v2, /device:TPU:27, one launch (start us, length us, event | category | flops | bytes accessed | tf_op | source)
XLA Modules:
  0.0 201.9 jit_solution(17585057037287780302)
XLA Ops:
  0.0 1.2 reshape.4.rates
  1.2 0.8 select_reduce_fusion.pairs
  2.1 0.0 copy-start
  2.1 0.6 dynamic_slice.3.lowers
  2.6 0.0 copy-done
  2.7 24.6 %shard_map.91.sent_ref = f32[3,32,3,24,128]{4,3,2,1,0:T(8,128)} custom-call(s32[24]{0:T(128)} %counts.3, s32[384]{0:T(512)} %copy-done, f32[384]{0:T(512)} %weights.1, f32[3,4,24,2,1536]{4,3,2,1,0:T(2,128)} %field_ref.1, f32[3,4,24,2,1536]{4,3,2,1,0:T(2,128)} %more_ref.1), custom_call_target="tpu_custom_call" | custom-call | flops 8153726976 | tf_op jit(solution)/shard_map/pallas_call | solution.py:472
  27.3 147.3 %shard_map.92.come_ref = f32[3,32,3,24,128]{4,3,2,1,0:T(8,128)} custom-call(s32[12]{0:T(128)} %dynamic_slice.3.lowers, f32[24]{0:T(128)} %reshape.4.rates, f32[3,32,3,24,128]{4,3,2,1,0:T(8,128)} %shard_map.91.sent_ref, f32[12,769,384]{2,1,0:T(8,128)} %bitcast.1, s32[1,256]{1,0:T(1,128)} %constant.20.clone.rank_ref, s32[1,256]{1,0:T(1,128)} %constant.21.clone.mine_ref), custom_call_target="tpu_custom_call" | custom-call | flops 12683575296 | tf_op jit(solution)/shard_map/pallas_call | solution.py:502
  174.6 27.3 %shard_map.93 = f32[3,4,24,2,1536]{4,3,2,1,0:T(2,128)} custom-call(s32[24]{0:T(128)} %counts.3, s32[384]{0:T(512)} %copy-done, f32[3,32,3,24,128]{4,3,2,1,0:T(8,128)} %shard_map.92.come_ref), custom_call_target="tpu_custom_call" | custom-call | flops 8153726976 | tf_op jit(solution)/shard_map/pallas_call | solution.py:540
Async XLA Ops:
  2.1 0.6 copy-start

commit v3 on v2

--- a/solution.py
+++ b/solution.py
@@ -67,12 +67,14 @@
     )
 
 
-def forward_kernel(
+def forward_step(
+    step, group_steps, finish,
     counts, pairs, weights, field_ref, more_ref, out_ref, row_ref, high_ref, low_ref, wave_ref,
-    *, stride,
+    *, stride, lats, sets,
 ):
     fields, local, _, _, length = field_ref.shape
-    chunks, devices, tiles, lats, _ = out_ref.shape
+    chunks, devices, tiles, _, _ = out_ref.shape
+    each_set = lats // sets
     waves = length // 2
     rows = fields * local * 2
     each = 2 * local
@@ -82,7 +84,7 @@
     each_step = field_ref.shape[2]
 
     def one(sub, carry):
-        lat = pl.program_id(0) * each_step + sub
+        lat = step * each_step + sub
         count = counts[lat]
         real = 2.0 * count.astype(jnp.float32)
         inverse = 1.0 / jnp.full((1, 1), real, jnp.float32)
@@ -141,23 +143,24 @@
                     [real_part[f * each : (f + 1) * each], imaginary[f * each : (f + 1) * each]], axis=0
                 )
             turned = jnp.concatenate(parts, axis=0).T
-            wave_ref[pl.ds(q * SPAN * stride + lat, SPAN, stride=stride), :] = turned
+            wave_ref[pl.ds(q * SPAN * stride + lat % each_set, SPAN, stride=stride), :] = turned
         return carry
 
     lax.fori_loop(0, each_step, one, 0, unroll=SUB)
 
-    @pl.when(pl.program_id(0) == pl.num_programs(0) - 1)
+    @pl.when(step % group_steps == group_steps - 1)
     def _():
-        lane = iota((lats, LANES), 1) // wide
+        part = step // group_steps
+        lane = iota((each_set, LANES), 1) // wide
 
         def assemble(index, carry):
             chunk, device = index // devices, index % devices
-            outs = [jnp.zeros((lats, LANES), jnp.float32)] * tiles
+            outs = [jnp.zeros((each_set, LANES), jnp.float32)] * tiles
             for s in range(group):
                 lower = pairs[device * chunks * group + chunk * group + s]
                 for member in range(2):
                     wave = lower if member == 0 else waves - 1 - lower
-                    value = wave_ref[pl.ds(wave * stride, lats), :]
+                    value = wave_ref[pl.ds(wave * stride, each_set), :]
                     moved = {}
                     for f in range(fields):
                         unit = member * fields + f
@@ -167,14 +170,34 @@
                             moved[step] = pltpu.roll(value, step, 1)
                         outs[unit // 2] = jnp.where(lane == spot, moved[step], outs[unit // 2])
             for t in range(tiles):
-                out_ref[chunk, device, t] = outs[t]
+                out_ref[chunk, device, t, pl.ds(part * each_set, each_set)] = outs[t]
             return carry
 
         lax.fori_loop(0, devices * chunks, assemble, 0, unroll=UNROLL)
+        finish(part)
+
+
+def inverse_tables(count, high_ref, low_ref):
+    real = 2.0 * count.astype(jnp.float32)
+    inverse = 1.0 / jnp.full((1, 1), real, jnp.float32)
+    place = 2.0 * iota((1, HALF_SPAN), 1).astype(jnp.float32) + 1.0
+    steps = iota((FINE, HALF_SPAN), 0).astype(jnp.float32)
+    fine_cos, fine_sin = turn(steps * place, real, inverse)
+    for q in range(high_ref.shape[1]):
+        coarse_cos, coarse_sin = turn((q * SPAN + FINE * steps) * place, real, inverse)
+        for i in range(SPAN // FINE):
+            cosine, sine = coarse_cos[i : i + 1], coarse_sin[i : i + 1]
+            part = pl.ds(i * FINE, FINE)
+            top, rest = halves(cosine * fine_cos - sine * fine_sin)
+            high_ref[0, q, 0, part] = top
+            low_ref[0, q, 0, part] = rest
+            top, rest = halves(sine * fine_cos + cosine * fine_sin)
+            high_ref[0, q, 1, part] = top
+            low_ref[0, q, 1, part] = rest
 
 
 def inverse_kernel(
-    counts, pairs, come_ref, out_ref, high_ref, low_ref, wave_ref, *, stride, light, short
+    counts, pairs, come_ref, high_ref, low_ref, out_ref, wave_ref, *, stride, light, short
 ):
     fields, local, _, _, length = out_ref.shape
     chunks, devices, tiles, lats, _ = come_ref.shape
@@ -222,24 +245,11 @@
         total = blocks * rows
         with_cos = jnp.zeros((total, HALF_SPAN), jnp.float32)
         with_sin = jnp.zeros((total, HALF_SPAN), jnp.float32)
-        place = 2.0 * iota((1, HALF_SPAN), 1).astype(jnp.float32) + 1.0
-        steps = iota((FINE, HALF_SPAN), 0).astype(jnp.float32)
-        fine_cos, fine_sin = turn(steps * place, real, inverse)
         for q in range(waves // SPAN):
             start = q * SPAN
-            coarse_cos, coarse_sin = turn((start + FINE * steps) * place, real, inverse)
             order = start + iota((1, SPAN), 1).astype(jnp.float32)
             rank = iota((8, SPAN), 0).astype(jnp.float32)
             block_cos, block_sin = turn((2 * SPAN * rank + (SPAN - 1)) * order, real, inverse)
-            for i in range(SPAN // FINE):
-                cosine, sine = coarse_cos[i : i + 1], coarse_sin[i : i + 1]
-                part = pl.ds(i * FINE, FINE)
-                top, rest = halves(cosine * fine_cos - sine * fine_sin)
-                high_ref[q, 0, part] = top
-                low_ref[q, 0, part] = rest
-                top, rest = halves(sine * fine_cos + cosine * fine_sin)
-                high_ref[q, 1, part] = top
-                low_ref[q, 1, part] = rest
             turned = wave_ref[pl.ds(q * SPAN * stride + lat, SPAN, stride=stride), :].T
             real_part = jnp.concatenate(
                 [turned[seat_of(f) * wide :][:each] for f in range(fields)], axis=0
@@ -257,11 +267,11 @@
                 evens.append(real_part * cosine - imaginary * sine)
                 odds.append(real_part * sine + imaginary * cosine)
             even, low = halves(jnp.concatenate(evens, axis=0))
-            first = dot(jnp.concatenate([even, low], axis=0), high_ref[q, 0])
-            with_cos += first[:total] + (first[total:] + dot(even, low_ref[q, 0]))
+            first = dot(jnp.concatenate([even, low], axis=0), high_ref[sub, q, 0])
+            with_cos += first[:total] + (first[total:] + dot(even, low_ref[sub, q, 0]))
             odd, low = halves(jnp.concatenate(odds, axis=0))
-            first = dot(jnp.concatenate([odd, low], axis=0), high_ref[q, 1])
-            with_sin += first[:total] + (first[total:] + dot(odd, low_ref[q, 1]))
+            first = dot(jnp.concatenate([odd, low], axis=0), high_ref[sub, q, 1])
+            with_sin += first[:total] + (first[total:] + dot(odd, low_ref[sub, q, 1]))
         right, left = with_cos - with_sin, reverse(with_cos + with_sin)
         for b in range(blocks):
             for part, side in ((0, left), (1, right)):
@@ -278,33 +288,50 @@
 
 
 def exchange_kernel(
-    lowers, rates, sent_ref, table_ref, rank_ref, mine_ref, home_ref,
-    come_ref, back_ref, pad_ref, data_ref, out_sem, in_sem, back_out_sem, back_in_sem, own_sem,
-    *, lev, waves, light, short,
+    counts, pairs, weights, lowers, rates, field_ref, more_ref, table_ref, rank_ref, mine_ref,
+    home_ref, top_ref, rest_ref, row_ref, high_ref, low_ref, wave_ref, sent_ref, come_ref, back_ref, pad_ref,
+    data_ref, out_sem, in_sem, back_out_sem, back_in_sem, own_sem,
+    *, lev, waves, light, short, stride, lat_steps, sets,
 ):
-    slot = pl.program_id(0)
+    step = pl.program_id(0)
+    slot = step - lat_steps
     chunks, devices, tiles, lats, _ = come_ref.shape
+    each_set = lats // sets
     bands = devices // lev
-    slots = pl.num_programs(0)
+    slots = pl.num_programs(0) - lat_steps - lats
     group = waves // 2 // devices // chunks
     chunk, spot = slot // group, slot % group
     band = lax.axis_index("band")
     me = band * lev + lax.axis_index("lev")
 
-    def message(source, target, send_sem, recv_sem, g, there, where, device, small):
-        part = pl.ds(0, short if small else tiles)
+    def copy(source, target, send_sem, recv_sem, device):
         return pltpu.make_async_remote_copy(
-            src_ref=source.at[g, there, part],
-            dst_ref=target.at[g, where, part],
-            send_sem=send_sem.at[g, there],
-            recv_sem=recv_sem.at[g, where],
+            src_ref=source,
+            dst_ref=target,
+            send_sem=send_sem,
+            recv_sem=recv_sem,
             device_id=(device // lev, device % lev),
             device_id_type=pl.DeviceIdType.MESH,
         )
 
+    def message(n, there, where, device, small, split):
+        part = pl.ds(0, short if small else tiles)
+        g, rows = (0, pl.ds(n * each_set, each_set)) if split else (n - sets + 1, pl.ds(0, lats))
+        return copy(
+            sent_ref.at[g, there, part, rows], come_ref.at[g, where, part, rows],
+            out_sem.at[n, there], in_sem.at[n, where], device,
+        )
+
+    def answer(g, there, where, device, small):
+        part = pl.ds(0, short if small else tiles)
+        return copy(
+            back_ref.at[g, there, part], home_ref.at[g, where, part],
+            back_out_sem.at[g, there], back_in_sem.at[g, where], device,
+        )
+
     def each_other(act, g, small_of):
-        def one(step, carry):
-            other = lax.rem(me + step, devices)
+        def one(hop, carry):
+            other = lax.rem(me + hop, devices)
             small = small_of(other)
 
             @pl.when(small)
@@ -325,119 +352,149 @@
     def their_small(other):
         return other // lev < light
 
-    def go(g, other, small):
-        message(sent_ref, come_ref, out_sem, in_sem, g, other, me, other, small).start()
-
-    def gone(g, other, small):
-        message(sent_ref, come_ref, out_sem, in_sem, g, other, me, other, small).wait_send()
-
-    def come(g, other, small):
-        message(sent_ref, come_ref, out_sem, in_sem, g, other, other, other, small).wait_recv()
-
     def back_go(g, other, small):
-        message(back_ref, home_ref, back_out_sem, back_in_sem, g, other, me, other, small).start()
+        answer(g, other, me, other, small).start()
 
     def back_gone(g, other, small):
-        message(back_ref, home_ref, back_out_sem, back_in_sem, g, other, me, other, small).wait_send()
+        answer(g, other, me, other, small).wait_send()
 
     def back_come(g, other, small):
-        message(
-            back_ref, home_ref, back_out_sem, back_in_sem, g, other, other, other, small
-        ).wait_recv()
-
-    def own(g):
-        return pltpu.make_async_copy(sent_ref.at[g, me], come_ref.at[g, me], own_sem.at[g])
+        answer(g, other, other, other, small).wait_recv()
 
     def own_back(g):
-        return pltpu.make_async_copy(
-            back_ref.at[g, me], home_ref.at[g, me], own_sem.at[chunks + g]
+        return pltpu.make_async_copy(back_ref.at[g, me], home_ref.at[g, me], own_sem.at[g])
+
+    def send(n, split):
+        def act(n, other, small):
+            message(n, other, me, other, small, split).start()
+
+        each_other(act, n, mine_small)
+
+    def arrive(n, split):
+        def act(n, other, small):
+            message(n, other, other, other, small, split).wait_recv()
+
+        each_other(act, n, their_small)
+
+    def leave(n, split):
+        def act(n, other, small):
+            message(n, other, me, other, small, split).wait_send()
+
+        each_other(act, n, mine_small)
+
+    def all_of(act, first, last, split):
+        lax.fori_loop(first, last, lambda n, carry: (act(n, split), carry)[1], 0)
+
+    def finish(part):
+        send(part, True)
+
+        @pl.when(part == sets - 1)
+        def _():
+            all_of(send, sets, sets + chunks - 1, False)
+
+    def legendre():
+        columns = table_ref.shape[1]
+        pad_ref[:columns] = table_ref[0]
+        table_high, table_low = halves(pad_ref[...])
+
+        @pl.when(slot == 0)
+        def _():
+            all_of(arrive, 0, sets, True)
+
+        @pl.when((slot > 0) & (spot == 0))
+        def _():
+            arrive(chunk + sets - 1, False)
+
+        arrays = lev * tiles
+        wides = -(-arrays // SEATS)
+        width = wides * LANES
+        member = LANES // (2 * SEATS)
+        seat = iota((lats, LANES), 1) // member % SEATS
+        for b in range(bands):
+            for w in range(wides):
+                value = jnp.zeros((lats, LANES), jnp.float32)
+                for k in range(w * SEATS, min((w + 1) * SEATS, arrays)):
+                    if b < light and k % tiles >= short:
+                        continue
+                    piece = come_ref[chunk, b * lev + k // tiles, k % tiles]
+                    shift = lax.rem((k % SEATS - spot) * member + LANES, LANES)
+                    value = jnp.where(seat == k % SEATS, pltpu.roll(piece, shift, 1), value)
+                rows = pl.ds(b * lats, lats)
+                data_ref[rows, w * LANES : (w + 1) * LANES] = value
+        high, low = halves(mirror(data_ref[...]))
+        first = dot(table_high, jnp.concatenate([high, low], axis=1))
+        analysed = first[:, :width] + (first[:, width:] + dot(table_low, high))
+        lower = lowers[slot]
+        column = iota((pad_ref.shape[0], 1), 0)
+        second = column >= waves - lower
+        degree = jnp.where(second, column - 1, lower + column)
+        order = jnp.where(second, waves - 1 - lower, lower)
+        odd = (degree - order) & 1
+        code = jnp.where(column <= waves, 2 * second.astype(jnp.int32) + odd, -1)
+        degree = degree.astype(jnp.float32)
+        ratio = degree * (degree + 1.0) * (1.0 / float((waves - 1) * waves))
+        square = ratio * ratio
+        rate = jnp.zeros(rank_ref.shape, jnp.float32)
+        for r in range(rates.shape[0]):
+            rate = jnp.where(rank_ref[...] == r, rates[r], rate)
+        damped = jnp.where(code == mine_ref[...], analysed / (1.0 + rate * square), 0.0)
+        high, low = halves(damped)
+        first = dot(table_high.T, jnp.concatenate([high, low], axis=1))
+        back = first[:, :width] + (first[:, width:] + dot(table_low.T, high))
+        data_ref[...] = mirror(back)
+
+        @pl.when(spot == 0)
+        def _():
+            back_ref[chunk] = jnp.zeros(back_ref.shape[1:], jnp.float32)
+
+        for b in range(bands):
+            for k in range(arrays):
+                if b < light and k % tiles >= short:
+                    continue
+                w = k // SEATS
+                piece = data_ref[pl.ds(b * lats, lats), w * LANES : (w + 1) * LANES]
+                shift = lax.rem((spot - k % SEATS) * member + LANES, LANES)
+                target = (chunk, b * lev + k // tiles, k % tiles)
+                back_ref[target] = jnp.where(seat == spot, pltpu.roll(piece, shift, 1), back_ref[target])
+
+        @pl.when(spot == group - 1)
+        def _():
+            own_back(chunk).start()
+            each_other(back_go, chunk, their_small)
+
+    @pl.when(step < lat_steps)
+    def _():
+        forward_step(
+            step, lat_steps // sets, finish,
+            counts, pairs, weights, field_ref, more_ref, sent_ref,
+            row_ref, high_ref, low_ref, wave_ref, stride=stride, lats=lats, sets=sets,
         )
 
     @pl.when(slot == 0)
     def _():
-        def begin(g, carry):
-            own(g).start()
-            each_other(go, g, mine_small)
-            return carry
-
-        lax.fori_loop(0, chunks, begin, 0)
         pad_ref[...] = jnp.zeros_like(pad_ref)
-
-    columns = table_ref.shape[1]
-    pad_ref[:columns] = table_ref[0]
-    table_high, table_low = halves(pad_ref[...])
-
-    @pl.when(spot == 0)
+        for g in range(chunks):
+            come_ref[g, me] = sent_ref[g, me]
+
+    @pl.when((slot >= 0) & (slot < slots))
     def _():
-        own(chunk).wait()
-        each_other(come, chunk, their_small)
-
-    arrays = lev * tiles
-    wides = -(-arrays // SEATS)
-    width = wides * LANES
-    member = LANES // (2 * SEATS)
-    seat = iota((lats, LANES), 1) // member % SEATS
-    for b in range(bands):
-        for w in range(wides):
-            value = jnp.zeros((lats, LANES), jnp.float32)
-            for k in range(w * SEATS, min((w + 1) * SEATS, arrays)):
-                if b < light and k % tiles >= short:
-                    continue
-                piece = come_ref[chunk, b * lev + k // tiles, k % tiles]
-                shift = lax.rem((k % SEATS - spot) * member + LANES, LANES)
-                value = jnp.where(seat == k % SEATS, pltpu.roll(piece, shift, 1), value)
-            data_ref[pl.ds(b * lats, lats), w * LANES : (w + 1) * LANES] = value
-    high, low = halves(mirror(data_ref[...]))
-    first = dot(table_high, jnp.concatenate([high, low], axis=1))
-    analysed = first[:, :width] + (first[:, width:] + dot(table_low, high))
-    lower = lowers[slot]
-    column = iota((pad_ref.shape[0], 1), 0)
-    second = column >= waves - lower
-    degree = jnp.where(second, column - 1, lower + column)
-    order = jnp.where(second, waves - 1 - lower, lower)
-    odd = (degree - order) & 1
-    code = jnp.where(column <= waves, 2 * second.astype(jnp.int32) + odd, -1)
-    degree = degree.astype(jnp.float32)
-    ratio = degree * (degree + 1.0) * (1.0 / float((waves - 1) * waves))
-    square = ratio * ratio
-    rate = jnp.zeros(rank_ref.shape, jnp.float32)
-    for r in range(rates.shape[0]):
-        rate = jnp.where(rank_ref[...] == r, rates[r], rate)
-    damped = jnp.where(code == mine_ref[...], analysed / (1.0 + rate * square), 0.0)
-    high, low = halves(damped)
-    first = dot(table_high.T, jnp.concatenate([high, low], axis=1))
-    back = first[:, :width] + (first[:, width:] + dot(table_low.T, high))
-    data_ref[...] = mirror(back)
-
-    @pl.when(spot == 0)
+        legendre()
+
+    @pl.when(slot >= slots)
     def _():
-        back_ref[chunk] = jnp.zeros(back_ref.shape[1:], jnp.float32)
-
-    for b in range(bands):
-        for k in range(arrays):
-            if b < light and k % tiles >= short:
-                continue
-            w = k // SEATS
-            piece = data_ref[pl.ds(b * lats, lats), w * LANES : (w + 1) * LANES]
-            shift = lax.rem((spot - k % SEATS) * member + LANES, LANES)
-            target = (chunk, b * lev + k // tiles, k % tiles)
-            back_ref[target] = jnp.where(seat == spot, pltpu.roll(piece, shift, 1), back_ref[target])
-
-    @pl.when(spot == group - 1)
-    def _():
-        own_back(chunk).start()
-        each_other(back_go, chunk, their_small)
-
-    @pl.when(slot == slots - 1)
+        inverse_tables(counts[slot - slots], top_ref, rest_ref)
+
+    @pl.when(slot == slots + lats - 1)
     def _():
         def end(g, carry):
             own_back(g).wait()
             each_other(back_come, g, mine_small)
-            each_other(gone, g, mine_small)
             each_other(back_gone, g, their_small)
             return carry
 
         lax.fori_loop(0, chunks, end, 0)
+        all_of(leave, 0, sets, True)
+        all_of(leave, sets, sets + chunks - 1, False)
 
 
 def body(field_grid, increment, points, weights, pair_slot, legendre, strength):
@@ -461,32 +518,22 @@
     ]
     light = sum((cells - 1) // 2 < pair_count for cells in most)
     stride = lats + 1 - lats % 2
+    each_set = 8 if lats % 8 == 0 else lats
+    sets = lats // each_set
+    set_stride = each_set + 1 - each_set % 2
     blocks = length // SPAN
     rows = fields * local * 2
-    each_step = max(g for g in range(1, EACH + 1) if lats % g == 0)
+    each_step = max(g for g in range(1, EACH + 1) if each_set % g == 0)
+    lat_steps = lats // each_step
     grid_block = pl.BlockSpec((fields, local, each_step, 2, length), lambda j, *_: (0, 0, j, 0, 0))
     buffer = (chunks, devices, tiles, lats, LANES)
+    early_block = pl.BlockSpec(
+        (fields, local, each_step, 2, length),
+        lambda s, *_: (0, 0, jnp.minimum(s, lat_steps - 1), 0, 0),
+    )
     whole_block = pl.BlockSpec(buffer, lambda j, *_: (0, 0, 0, 0, 0))
     waved = pltpu.VMEM((waves * stride, LANES), jnp.float32)
     flops = lats * 6 * blocks * rows * SPAN * length
-    sent = pl.pallas_call(
-        functools.partial(forward_kernel, stride=stride),
-        out_shape=jax.ShapeDtypeStruct(buffer, jnp.float32),
-        grid_spec=pltpu.PrefetchScalarGridSpec(
-            num_scalar_prefetch=3,
-            grid=(lats // each_step,),
-            in_specs=[grid_block, grid_block],
-            out_specs=whole_block,
-            scratch_shapes=[
-                pltpu.VMEM((rows, length), jnp.float32),
-                pltpu.VMEM((waves // SPAN, HALF_SPAN, 2 * SPAN), jnp.bfloat16),
-                pltpu.VMEM((waves // SPAN, HALF_SPAN, 2 * SPAN), jnp.bfloat16),
-                waved,
-            ],
-        ),
-        cost_estimate=pl.CostEstimate(flops=flops, bytes_accessed=0, transcendentals=0),
-    )(points, pairs, weights, field_grid, increment)
-
     arrays = lev * tiles
     width = -(-arrays // SEATS) * LANES
     padded = -(-columns // LANES) * LANES
@@ -499,29 +546,49 @@
     level = array // tiles * local + lane // 2 % local
     rank = np.where(real, unit % fields * lev * local + level, 0)
     own = lax.dynamic_slice_in_dim(pairs, lax.axis_index(("band", "lev")) * slots, slots)
-    home = pl.pallas_call(
-        functools.partial(exchange_kernel, lev=lev, waves=waves, light=light, short=short),
-        out_shape=jax.ShapeDtypeStruct(buffer, jnp.float32),
+    turns = (waves // SPAN, 2, SPAN, HALF_SPAN)
+    home, top, rest = pl.pallas_call(
+        functools.partial(
+            exchange_kernel, lev=lev, waves=waves, light=light, short=short,
+            stride=set_stride, lat_steps=lat_steps, sets=sets,
+        ),
+        out_shape=[jax.ShapeDtypeStruct(buffer, jnp.float32)]
+        + [jax.ShapeDtypeStruct((lats, *turns), jnp.bfloat16)] * 2,
         grid_spec=pltpu.PrefetchScalarGridSpec(
-            num_scalar_prefetch=2,
-            grid=(slots,),
+            num_scalar_prefetch=5,
+            grid=(lat_steps + slots + lats,),
             in_specs=[
-                pl.BlockSpec(memory_space=pl.ANY),
-                pl.BlockSpec((1, columns, half), lambda s, *_: (s, 0, 0)),
+                early_block,
+                early_block,
+                pl.BlockSpec(
+                    (1, columns, half), lambda s, *_: (jnp.clip(s - lat_steps, 0, slots - 1), 0, 0)
+                ),
                 pl.BlockSpec((1, width), lambda s, *_: (0, 0)),
                 pl.BlockSpec((1, width), lambda s, *_: (0, 0)),
             ],
-            out_specs=pl.BlockSpec(memory_space=pl.ANY),
+            out_specs=[pl.BlockSpec(memory_space=pl.ANY)]
+            + [
+                pl.BlockSpec(
+                    (1, *turns),
+                    lambda s, *_: (jnp.maximum(s - lat_steps - slots, 0), 0, 0, 0, 0),
+                )
+            ]
+            * 2,
             scratch_shapes=[
+                pltpu.VMEM((rows, length), jnp.float32),
+                pltpu.VMEM((waves // SPAN, HALF_SPAN, 2 * SPAN), jnp.bfloat16),
+                pltpu.VMEM((waves // SPAN, HALF_SPAN, 2 * SPAN), jnp.bfloat16),
+                pltpu.VMEM((waves * set_stride, LANES), jnp.float32),
+                pltpu.VMEM(buffer, jnp.float32),
                 pltpu.VMEM(buffer, jnp.float32),
                 pltpu.VMEM(buffer, jnp.float32),
                 pltpu.VMEM((padded, half), jnp.float32),
                 pltpu.VMEM((half, width), jnp.float32),
+                pltpu.SemaphoreType.DMA((sets + chunks - 1, devices)),
+                pltpu.SemaphoreType.DMA((sets + chunks - 1, devices)),
                 pltpu.SemaphoreType.DMA((chunks, devices)),
                 pltpu.SemaphoreType.DMA((chunks, devices)),
-                pltpu.SemaphoreType.DMA((chunks, devices)),
-                pltpu.SemaphoreType.DMA((chunks, devices)),
-                pltpu.SemaphoreType.DMA((2 * chunks,)),
+                pltpu.SemaphoreType.DMA((chunks,)),
             ],
         ),
         compiler_params=pltpu.CompilerParams(has_side_effects=True),
@@ -529,9 +596,13 @@
             flops=slots * 12 * half * padded * width, bytes_accessed=0, transcendentals=0
         ),
     )(
+        points,
+        pairs,
+        weights,
         own,
         strength.reshape(-1),
-        sent,
+        field_grid,
+        increment,
         jnp.swapaxes(legendre, 1, 2),
         jnp.asarray(rank[None, :], jnp.int32),
         jnp.asarray(mine[None, :], jnp.int32),
@@ -543,16 +614,15 @@
         grid_spec=pltpu.PrefetchScalarGridSpec(
             num_scalar_prefetch=2,
             grid=(lats // each_step,),
-            in_specs=[whole_block],
+            in_specs=[whole_block]
+            + [pl.BlockSpec((each_step, *turns), lambda j, *_: (j, 0, 0, 0, 0))] * 2,
             out_specs=grid_block,
             scratch_shapes=[
-                pltpu.VMEM((waves // SPAN, 2, SPAN, HALF_SPAN), jnp.bfloat16),
-                pltpu.VMEM((waves // SPAN, 2, SPAN, HALF_SPAN), jnp.bfloat16),
                 waved,
             ],
         ),
         cost_estimate=pl.CostEstimate(flops=flops, bytes_accessed=0, transcendentals=0),
-    )(points, pairs, home)
+    )(points, pairs, home, top, rest)
 
 
 def solution(mesh):

time: 202 us -> 193 us (0.955)
  Pallas kernels: 199 us -> 190 us
    pallas_call x1 -> x0, Pallas kernels: 24.6 us -> none  [body(): pl.pallas_call(functools.partial(forward_kernel, stride=stride), out_shap...]
    pallas_call x1, Pallas kernels: 147 us -> 167 us  [body(): pl.pallas_call(functools.partial(exchange_kernel, lev=lev, waves=waves, l...]
    pallas_call x1, Pallas kernels: 27.3 us -> 23.2 us  [body(): pl.pallas_call(functools.partial(inverse_kernel, stride=stride, light=lig...]
where the time goes in v3:
time: 193 us
  Pallas kernels  190 us (98%)
  local copies, waits for them, and re-layouts  1.94 us (1%)
    pallas_call x1, Pallas kernels, body(): pl.pallas_call(functools.partial(exchange_kernel, lev=lev, waves=waves, l...  167 us
    pallas_call x1, Pallas kernels, body(): pl.pallas_call(functools.partial(inverse_kernel, stride=stride, light=lig...  23.2 us

profile of v3, /device:TPU:27, one launch (start us, length us, event | category | flops | bytes accessed | tf_op | source)
XLA Modules:
  0.0 192.9 jit_solution(4926250327880787524)
XLA Ops:
  0.0 1.3 reshape.4.rates
  1.3 0.8 select_reduce_fusion.pairs
  2.2 0.0 copy-start
  2.2 0.6 dynamic_slice.3.lowers
  2.8 0.0 copy-done
  2.8 167.0 %shard_map.91 = (f32[3,32,3,24,128]{4,3,2,1,0:T(8,128)}, bf16[24,3,2,256,128]{4,3,2,1,0:T(8,128)(2,1)}, bf16[24,3,2,256,128]{4,3,2,1,0:T(8,128)(2,1)}) custom-call(s32[24]{0:T(128)} %counts.3, s32[384]{0:T(512)} %copy-done, f32[384]{0:T(512)} %weights.1, s32[12]{0:T(128)} %dynamic_slice.3.lowers, f32[24]{0:T(128)} %reshape.4.rates, ...), custom_call_target="tpu_custom_call" | custom-call | flops 12683575296 | tf_op jit(solution)/shard_map/pallas_call | solution.py:550
  169.8 23.2 %shard_map.92 = f32[3,4,24,2,1536]{4,3,2,1,0:T(2,128)} custom-call(s32[24]{0:T(128)} %counts.3, s32[384]{0:T(512)} %copy-done, f32[3,32,3,24,128]{4,3,2,1,0:T(8,128)} %get-tuple-element.8.come_ref, bf16[24,3,2,256,128]{4,3,2,1,0:T(8,128)(2,1)} %get-tuple-element.9.high_ref, bf16[24,3,2,256,128]{4,3,2,1,0:T(8,128)(2,1)} %get-tuple-element.10.low_ref), custom_call_target="tpu_custom_call" | custom-call | flops 8153726976 | tf_op jit(solution)/shard_map/pallas_call | solution.py:611
Async XLA Ops:
  2.2 0.6 copy-start
